TPU v7x, 256 devices: a whole 4x4x8 slice. The times are simulated.
256 devices in a mesh: level: 32 (over z, y), bal: 8 (over x, core).
Axes of the slice: x: 4, y: 4, z: 8, core: 2. Of those that a mesh axis runs over, the one named last changes fastest.
Arguments:
- patches: float32 [6144, 5, 4096], P(('level', 'bal')), may hold values from -6 to 6
- patch_ids: int32 [6144], P(('level', 'bal')), may hold values from 0 to 6143, each once
- live: int32 [256], P(('level', 'bal')), may hold values from 4 to 12, as said below
- counts: int32 [3, 256], P(None, ('level', 'bal')), may hold values from 0 to 4, as said below
- parent_of: int32 [6144], replicated, may hold values from 0 to 63
Outputs:
- new_patches: float32 [6144, 5, 4096], P(('level', 'bal'))
- new_ids: int32 [6144], P(('level', 'bal'))
- coarse: float32 [64, 5, 512], P('level')
Inputs may be any that keep to these rules, and one draw needn't show every extreme that they name: In every level group one device holds exactly 12 live patches. counts[r, d] never exceeds the live patches of device d at the start of round r; in every round and level group some device sends exactly 4.
All inputs are finite; a program needn't handle non-finite values.
Results may differ from a plain program's by a relative error of at most 0.0003.
Values sent between devices are 32-bit elements; how exact they have to be, the bound alone decides.
No kernel may reach another device: no remote copies, remote signals or barrier semaphores. Data moves between devices by JAX's collectives and lax.ppermute only.
A program may use at most 64 MiB of HBM per device.

v0:
```python
import jax
import jax.numpy as jnp
from jax import lax
from jax.sharding import PartitionSpec as P

EDGE = 16
VARS = 5
SEND_MOST = 4
PAR_DEV = 2


def from_partner(array, axis, stride):
    return lax.ppermute(array, axis, [(i, i ^ 1 << stride) for i in range(lax.axis_size(axis))])


def in_blocks(array, dim, devices):
    before, after = (array.shape[:dim], array.shape[dim + 1 :])
    return jnp.moveaxis(array.reshape(*before, devices, -1, *after), dim, 0)


def sum_at_owner(array, axis, dim):
    devices = lax.axis_size(axis)
    tiles = lax.all_to_all(in_blocks(array, dim, devices), axis, 0, 0, tiled=True)
    return jnp.sum(tiles, axis=0)


def sent_to_all(array, axis):
    copies = jnp.broadcast_to(array, (lax.axis_size(axis), *array.shape))
    return lax.all_to_all(copies, axis, split_axis=0, concat_axis=0, tiled=True)


def over_copies(array, axis):
    return sent_to_all(array, axis).sum(axis=0)


def restrict(fine_rows):
    leading = fine_rows.shape[:-1]
    half_edge = EDGE // 2
    blocks = fine_rows.reshape(leading + (half_edge, 2, half_edge, 2, half_edge, 2))
    return jnp.mean(blocks, axis=(-5, -3, -1)).reshape(
        leading + (half_edge * half_edge * half_edge,)
    )


def take_top(fine_rows, fine_ids, held_count, sent_count):
    capacity = fine_rows.shape[0]
    lane_index = jnp.arange(SEND_MOST, dtype=jnp.int32)
    pick_index = jnp.clip(held_count - sent_count + lane_index, 0, capacity - 1)
    is_valid = lane_index < sent_count
    return (
        jnp.where(is_valid[:, None, None], fine_rows[pick_index], 0.0),
        jnp.where(is_valid, fine_ids[pick_index], -1),
    )


def place_rows(fine_rows, fine_ids, kept_count, in_rows, in_ids):
    capacity = fine_rows.shape[0]
    slot_index = jnp.arange(capacity, dtype=jnp.int32)
    offset = slot_index - kept_count
    is_hit = (offset >= 0) & (offset < SEND_MOST)
    place_index = jnp.clip(offset, 0, SEND_MOST - 1)
    is_kept = slot_index < kept_count
    new_rows = jnp.where(
        is_kept[:, None, None],
        fine_rows,
        jnp.where(is_hit[:, None, None], in_rows[place_index], 0.0),
    )
    new_ids = jnp.where(is_kept, fine_ids, jnp.where(is_hit, in_ids[place_index], -1))
    return (new_rows, new_ids)


def pairwise_move(fine_rows, fine_ids, held_count, counts, rounds):
    for turn_index in range(rounds):
        sent_count = counts[turn_index, 0]
        out_rows, out_ids = take_top(fine_rows, fine_ids, held_count, sent_count)
        in_rows, in_marks = from_partner((out_rows, out_ids.astype(jnp.float32)), "bal", turn_index)
        in_ids = in_marks.astype(jnp.int32)
        kept_count = held_count - sent_count
        fine_rows, fine_ids = place_rows(fine_rows, fine_ids, kept_count, in_rows, in_ids)
        held_count = kept_count + jnp.sum((in_ids >= 0).astype(jnp.int32))
    return (fine_rows, fine_ids)


def parent_sums(fine_rows, fine_ids, parent_of):
    capacity = fine_rows.shape[0]
    reduced = restrict(fine_rows).reshape(capacity, -1)
    parent = jnp.where(fine_ids >= 0, parent_of[jnp.clip(fine_ids, 0, parent_of.shape[0] - 1)], -1)
    wanted = jnp.arange(PAR_DEV * lax.axis_size("level"), dtype=jnp.int32)
    one_hot = (wanted[:, None] == parent[None, :]).astype(jnp.float32)
    level_sums = sum_at_owner(
        jnp.dot(one_hot, reduced, precision=lax.Precision.HIGHEST), "level", 0
    )
    group_sums = over_copies(level_sums, "bal")
    return group_sums.reshape(PAR_DEV, VARS, -1)


def per_device(patches, patch_ids, live, counts, parent_of):
    capacity = patches.shape[0]
    group = lax.axis_size("bal")
    rounds = group.bit_length() - 1
    slot_index = jnp.arange(capacity, dtype=jnp.int32)
    held_count = live[0]
    is_kept = slot_index < held_count
    fine_rows = jnp.where(is_kept[:, None, None], patches, 0.0)
    fine_ids = jnp.where(is_kept, patch_ids, -1)
    coarse = parent_sums(fine_rows, fine_ids, parent_of)
    fine_rows, fine_ids = pairwise_move(fine_rows, fine_ids, held_count, counts, rounds)
    return (fine_rows, fine_ids, coarse)


def solution(mesh):
    return jax.shard_map(
        per_device,
        mesh=mesh,
        in_specs=(
            P(("level", "bal"), None, None),
            P(("level", "bal")),
            P(("level", "bal")),
            P(None, ("level", "bal")),
            P(),
        ),
        out_specs=(P(("level", "bal"), None, None), P(("level", "bal")), P("level", None, None)),
        check_vma=False,
    )
```

profile of v0, /device:TPU:1, one launch (start us, length us, event | category | flops | bytes accessed | tf_op | source)
XLA Modules:
  0.0 127.7 jit_solution(15075195029717672988)
XLA Ops:
  0.6 0.0 copy-start
  0.6 1.4 %fusion.19 = (s32[1,1]{0,1:T(1,128)}, s32[1,1]{0,1:T(1,128)}, s32[1,1]{0,1:T(1,128)}) fusion(s32[3,1]{0,1:T(1,128)} %param.8), kind=kLoop, calls=%fused_computation.79 | loop fusion | bytes 24 | tf_op jit(solution)/shard_map/slice | solution.py:74
  2.7 0.7 iota_compare_fusion.5
  4.0 0.0 copy-start.2
  4.0 4.7 %copy_select_fusion = f32[24,5,4096]{2,1,0:T(8,128)} fusion(f32[24,5,4096]{2,0,1:T(8,128)} %param.5, pred[24]{0:T(512)(128)(4,1)S(1)} %iota_compare_fusion.4), kind=kLoop, calls=%fused_computation.10 | loop fusion | flops 491520 | bytes 3932184 | tf_op jit(solution)/shard_map/jit(_where)/select_n | solution.py:104
  8.7 2.5 %gather_fusion.2 = f32[4,5,4096]{2,1,0:T(8,128)S(1)} fusion(f32[24,5,4096]{2,1,0:T(8,128)} %copy_select_fusion, s32[1024]{0:T(1024)S(1)} %pad_clamp_fusion.6), kind=kCustom, calls=%fused_computation.2 | custom fusion | bytes 655376 | tf_op jit(solution)/shard_map/gather | solution.py:51
  11.2 0.9 broadcast_select_fusion.2
  12.1 3.2 %collective-permute-start.2 = (f32[4,5,4096]{2,1,0:T(8,128)}, f32[4,5,4096]{2,1,0:T(8,128)S(1)}, u32[]{:S(2)}, u32[]{:S(2)}) collective-permute-start(f32[4,5,4096]{2,1,0:T(8,128)} %broadcast_select_fusion.2), channel_id=1, source_target_pairs={{0,1},{1,0},{2,3},{3,2},{4,5},{5,4},{6,7},{7,6},{8,9},{9,8},{10,11... | collective-permute-start | bytes 983048 | tf_op jit(solution)/shard_map/ppermute | solution.py:13
  15.3 0.0 copy-done.2
  15.3 0.6 gather_fusion
  16.0 0.7 select_convert_fusion.2
  16.6 0.1 collective-permute-start
  16.7 7.2 %copy.30 = f32[24,5,4096]{0,2,1:T(8,128)} copy(f32[24,5,4096]{2,1,0:T(8,128)} %copy_select_fusion) | data formatting | bytes 3932160 | tf_op jit(solution)/shard_map/jit(_where)/select_n | solution.py:104
  24.0 0.6 iota_compare_fusion.3
  24.6 0.7 iota_compare_fusion
  25.3 10.6 %reduce_sum.47 = f32[24,5,8,8,8]{0,4,3,2,1:T(8,128)S(1)} reduce(f32[24,5,8,2,8,2,8,2]{0,7,6,5,4,3,2,1:T(2,128)} %bitcast.45, f32[]{:T(128)} %constant.7.clone.1), dimensions={3,5,7}, to_apply=%region_2.3 | reduce | flops 430080 | bytes 2211844 | tf_op jit(solution)/shard_map/reduce_sum | solution.py:40
  35.9 0.2 broadcast_multiply_fusion
  36.0 0.0 copy-done
  36.0 0.7 gather_fusion.9
  36.7 0.0 collective-permute-done
  36.7 0.6 fusion.9
  38.7 0.7 fusion.20
  39.4 2.5 %compare_select_fusion.16 = (s32[24]{0:T(128)S(1)}, s32[24]{0:T(128)S(1)}) fusion(s32[24]{0:T(128)S(1)} %gather_fusion.9, s32[24]{0:T(128)S(1)} %get-tuple-element.19, s32[]{:T(128)} %bitcast.8, s32[]{:T(128)} %bitcast.7, s32[]{:T(128)} %bitcast.6, s32[]{:T(128)} %bitcast.5, s32[]{:T(128)S(6)} %sub.63), kind=kLoop, calls=%fused_computation.45 | loop fusion | flops 480 | bytes 404 | tf_op jit(solution)/shard_map/jit(_where)/select_n | solution.py:87
  41.9 0.6 gather_fusion.1
  42.6 0.6 select_convert_fusion.1
  43.2 0.1 collective-permute-start.1
  43.3 1.0 fusion
  44.3 1.3 %copy.32 = f32[32,2,2560]{2,1,0:T(2,128)} copy(f32[32,2,2560]{2,0,1:T(8,128)S(1)} %fusion) | data formatting | bytes 1310720 | tf_op jit(solution)/shard_map/dot_general | solution.py:91
  45.6 10.7 %all-to-all-start = ((f32[32,2,2560]{2,1,0:T(2,128)}), f32[32,2,2560]{2,1,0:T(2,128)S(1)}, u32[]{:S(2)}, u32[]{:S(2)}) async-start(f32[32,2,2560]{2,1,0:T(2,128)} %copy.32), calls=%async_computation | async-start | bytes 1310720 | tf_op jit(solution)/shard_map/all_to_all | solution.py:23
  56.4 0.0 collective-permute-done.1
  56.4 0.6 fusion.10
  58.3 0.6 fusion.18
  58.9 2.4 %fusion.6 = s32[24]{0:T(128)S(1)} fusion(s32[24]{0:T(128)S(1)} %get-tuple-element.21, s32[]{:T(128)} %bitcast.14, s32[]{:T(128)} %bitcast.15, s32[]{:T(128)} %bitcast.16, s32[]{:T(128)} %bitcast.17, s32[]{:T(128)S(6)} %sub.64), kind=kLoop, calls=%fused_computation.55 | loop fusion | flops 432 | bytes 212 | tf_op jit(solution)/shard_map/jit(_where)/select_n | solution.py:68
  61.4 0.6 gather_fusion.8
  62.0 0.7 select_convert_fusion
  62.7 0.0 copy-start.1
  62.7 2.5 %collective-permute-start.5 = (f32[4]{0:T(128)S(1)}, f32[4]{0:T(128)S(1)}, u32[]{:S(2)}, u32[]{:S(2)}) collective-permute-start(f32[4]{0:T(128)S(1)} %select_convert_fusion), channel_id=1, source_target_pairs={{0,4},{1,5},{2,6},{3,7},{4,0},{5,1},{6,2},{7,3},{8,12},{9,13},{10,... | collective-permute-start | bytes 56 | tf_op jit(solution)/shard_map/ppermute | solution.py:13
  65.2 0.0 collective-permute-done.2
  65.2 2.4 %gather_fusion.3 = f32[24,5,4096]{2,1,0:T(8,128)} fusion(f32[4,5,4096]{2,1,0:T(8,128)S(1)} %collective-permute-done.2, s32[1024]{0:T(1024)S(1)} %pad_clamp_fusion.4), kind=kCustom, calls=%fused_computation.3 | custom fusion | bytes 3932256 | tf_op jit(solution)/shard_map/gather | solution.py:66
  67.7 0.0 copy-done.1
  67.7 5.4 %select_select_fusion.2 = f32[24,5,4096]{2,1,0:T(8,128)} fusion(f32[24,5,4096]{2,1,0:T(8,128)} %gather_fusion.3, pred[24]{0:T(512)(128)(4,1)S(1)} %get-tuple-element.37, pred[24]{0:T(512)(128)(4,1)S(1)} %get-tuple-element.38, f32[24,5,4096]{2,0,1:T(8,128)S(1)} %copy-done.1, pred[24]{0:T(512)(128)(4,1)S(1)} %iota_compare_fusion.4), kind=kLoop, calls=%fused_computation.13 | loop fusion | flops 1474560 | bytes 5898312 | tf_op jit(solution)/shard_map/jit(_where)/select_n | solution.py:63
  73.1 2.5 %gather_fusion.4 = f32[4,5,4096]{2,1,0:T(8,128)S(1)} fusion(f32[24,5,4096]{2,1,0:T(8,128)} %select_select_fusion.2, s32[1024]{0:T(1024)S(1)} %pad_clamp_fusion.5), kind=kCustom, calls=%fused_computation.4 | custom fusion | bytes 655376 | tf_op jit(solution)/shard_map/gather | solution.py:51
  75.6 0.1 broadcast_select_fusion.1
  75.7 0.1 collective-permute-start.3
  75.8 0.0 collective-permute-done.5
  75.8 12.1 %collective-permute-done.3 = f32[4,5,4096]{2,1,0:T(8,128)S(1)} collective-permute-done((f32[4,5,4096]{2,1,0:T(8,128)S(1)}, f32[4,5,4096]{2,1,0:T(8,128)S(1)}, u32[]{:S(2)}, u32[]{:S(2)}) %collective-permute-start.3) | collective-permute-done | bytes 327712 | tf_op jit(solution)/shard_map/ppermute | solution.py:13
  87.9 2.4 %gather_fusion.5 = f32[24,5,4096]{2,1,0:T(8,128)} fusion(f32[4,5,4096]{2,1,0:T(8,128)S(1)} %collective-permute-done.3, s32[1024]{0:T(1024)S(1)} %pad_clamp_fusion.3), kind=kCustom, calls=%fused_computation.5 | custom fusion | bytes 3932256 | tf_op jit(solution)/shard_map/gather | solution.py:66
  90.3 5.4 %select_select_fusion.1 = f32[24,5,4096]{2,1,0:T(8,128)} fusion(f32[24,5,4096]{2,1,0:T(8,128)} %select_select_fusion.2, f32[24,5,4096]{2,1,0:T(8,128)} %gather_fusion.5, pred[24]{0:T(512)(128)(4,1)S(1)} %get-tuple-element.39, pred[24]{0:T(512)(128)(4,1)S(1)} %get-tuple-element.40), kind=kLoop, calls=%fused_computation.12 | loop fusion | flops 983040 | bytes 5898288 | tf_op jit(solution)/shard_map/jit(_where)/select_n | solution.py:63
  95.8 2.5 %gather_fusion.6 = f32[4,5,4096]{2,1,0:T(8,128)S(1)} fusion(f32[24,5,4096]{2,1,0:T(8,128)} %select_select_fusion.1, s32[1024]{0:T(1024)S(1)} %pad_clamp_fusion.2), kind=kCustom, calls=%fused_computation.6 | custom fusion | bytes 655376 | tf_op jit(solution)/shard_map/gather | solution.py:51
  98.2 0.1 broadcast_select_fusion
  98.3 0.8 collective-permute-start.4
  99.1 0.7 fusion.17
  99.8 5.5 %fusion.8 = s32[24]{0:T(128)} fusion(s32[]{:T(128)} %bitcast.18, s32[]{:T(128)} %bitcast.19, s32[]{:T(128)} %bitcast.20, s32[]{:T(128)} %bitcast.21, s32[]{:T(128)S(6)} %sub.67, s32[24]{0:T(128)S(1)} %get-tuple-element.21, s32[]{:T(128)} %bitcast.17, s32[]{:T(128)} %bitcast.16, s32[]{:T(128)} %bitcast.15, s32[]{:T(128)} %bitcast.14, s32[]{:T(128)S(6)} %sub.64), kind=kLoop, calls=%fused_computation.57 | loop fusion | flops 864 | bytes 232 | tf_op jit(solution)/shard_map/jit(_where)/select_n | solution.py:68
  105.2 6.2 %collective-permute-done.4 = f32[4,5,4096]{2,1,0:T(8,128)S(1)} collective-permute-done((f32[4,5,4096]{2,1,0:T(8,128)S(1)}, f32[4,5,4096]{2,1,0:T(8,128)S(1)}, u32[]{:S(2)}, u32[]{:S(2)}) %collective-permute-start.4) | collective-permute-done | bytes 327712 | tf_op jit(solution)/shard_map/ppermute | solution.py:13
  111.4 2.4 %gather_fusion.7 = f32[24,5,4096]{2,1,0:T(8,128)} fusion(f32[4,5,4096]{2,1,0:T(8,128)S(1)} %collective-permute-done.4, s32[1024]{0:T(1024)S(1)} %pad_clamp_fusion.1), kind=kCustom, calls=%fused_computation.7 | custom fusion | bytes 3932256 | tf_op jit(solution)/shard_map/gather | solution.py:66
  113.8 0.0 all-to-all-done
  113.8 0.2 reduce_sum.48
  114.0 0.7 broadcast_in_dim.131
  114.7 6.3 %all-to-all-start.1 = ((f32[8,2,2560]{2,1,0:T(2,128)}), f32[8,2,2560]{2,1,0:T(2,128)S(1)}, u32[]{:S(2)}, u32[]{:S(2)}) async-start(f32[8,2,2560]{2,1,0:T(2,128)} %broadcast_in_dim.131), calls=%async_computation.1 | async-start | bytes 327680 | tf_op jit(solution)/shard_map/all_to_all | solution.py:29
  121.1 3.6 %select_select_fusion = f32[24,5,4096]{2,1,0:T(8,128)S(1)} fusion(f32[24,5,4096]{2,1,0:T(8,128)} %select_select_fusion.1, f32[24,5,4096]{2,1,0:T(8,128)} %gather_fusion.7, pred[24]{0:T(512)(128)(4,1)S(1)} %get-tuple-element.41, pred[24]{0:T(512)(128)(4,1)S(1)} %get-tuple-element.42), kind=kLoop, calls=%fused_computation.11 | loop fusion | flops 983040 | bytes 5898288 | tf_op jit(solution)/shard_map/jit(_where)/select_n | solution.py:63
  124.7 2.4 %copy.34 = f32[24,5,4096]{2,0,1:T(8,128)} copy(f32[24,5,4096]{2,1,0:T(8,128)S(1)} %select_select_fusion) | data formatting | bytes 3932160
  127.1 0.0 all-to-all-done.1
  127.1 0.7 reduce_sum.49
  (22 shorter events, 0.1 us)
Async XLA Ops:
  0.6 35.4 %copy-start = (s32[6144]{0:T(1024)S(1)}, s32[6144]{0:T(1024)}, u32[]{:S(2)}) copy-start(s32[6144]{0:T(1024)} %param.9) | copy-start | bytes 73732
  4.0 11.3 %copy-start.2 = (s32[24]{0:T(128)S(1)}, s32[24]{0:T(128)}, u32[]{:S(2)}) copy-start(s32[24]{0:T(128)} %param.6) | copy-start | bytes 292
  12.1 53.1 %collective-permute-start.2 = (f32[4,5,4096]{2,1,0:T(8,128)}, f32[4,5,4096]{2,1,0:T(8,128)S(1)}, u32[]{:S(2)}, u32[]{:S(2)}) collective-permute-start(f32[4,5,4096]{2,1,0:T(8,128)} %broadcast_select_fusion.2), channel_id=1, source_target_pairs={{0,1},{1,0},{2,3},{3,2},{4,5},{5,4},{6,7},{7,6},{8,9},{9,8},{10,11... | collective-permute-start | bytes 983048 | tf_op jit(solution)/shard_map/ppermute | solution.py:13
  16.6 20.1 %collective-permute-start = (f32[4]{0:T(128)S(1)}, f32[4]{0:T(128)S(1)}, u32[]{:S(2)}, u32[]{:S(2)}) collective-permute-start(f32[4]{0:T(128)S(1)} %select_convert_fusion.2), channel_id=1, source_target_pairs={{0,1},{1,0},{2,3},{3,2},{4,5},{5,4},{6,7},{7,6},{8,9},{9,8},{10,11... | collective-permute-start | bytes 56 | tf_op jit(solution)/shard_map/ppermute | solution.py:13
  43.2 13.1 %collective-permute-start.1 = (f32[4]{0:T(128)S(1)}, f32[4]{0:T(128)S(1)}, u32[]{:S(2)}, u32[]{:S(2)}) collective-permute-start(f32[4]{0:T(128)S(1)} %select_convert_fusion.1), channel_id=1, source_target_pairs={{0,2},{1,3},{2,0},{3,1},{4,6},{5,7},{6,4},{7,5},{8,10},{9,11},{10,... | collective-permute-start | bytes 56 | tf_op jit(solution)/shard_map/ppermute | solution.py:13
  45.6 68.2 %all-to-all-start = ((f32[32,2,2560]{2,1,0:T(2,128)}), f32[32,2,2560]{2,1,0:T(2,128)S(1)}, u32[]{:S(2)}, u32[]{:S(2)}) async-start(f32[32,2,2560]{2,1,0:T(2,128)} %copy.32), calls=%async_computation | async-start | bytes 1310720 | tf_op jit(solution)/shard_map/all_to_all | solution.py:23
  62.7 5.0 %copy-start.1 = (f32[24,5,4096]{2,0,1:T(8,128)S(1)}, f32[24,5,4096]{2,0,1:T(8,128)}, u32[]{:S(2)}) copy-start(f32[24,5,4096]{2,0,1:T(8,128)} %param.5) | copy-start | bytes 5898244
  62.7 13.1 %collective-permute-start.5 = (f32[4]{0:T(128)S(1)}, f32[4]{0:T(128)S(1)}, u32[]{:S(2)}, u32[]{:S(2)}) collective-permute-start(f32[4]{0:T(128)S(1)} %select_convert_fusion), channel_id=1, source_target_pairs={{0,4},{1,5},{2,6},{3,7},{4,0},{5,1},{6,2},{7,3},{8,12},{9,13},{10,... | collective-permute-start | bytes 56 | tf_op jit(solution)/shard_map/ppermute | solution.py:13
  75.7 12.2 %collective-permute-start.3 = (f32[4,5,4096]{2,1,0:T(8,128)S(1)}, f32[4,5,4096]{2,1,0:T(8,128)S(1)}, u32[]{:S(2)}, u32[]{:S(2)}) collective-permute-start(f32[4,5,4096]{2,1,0:T(8,128)S(1)} %broadcast_select_fusion.1), channel_id=1, source_target_pairs={{0,2},{1,3},{2,0},{3,1},{4,6},{5,7},{6,4},{7,5},{8,10},{9,11},{10,... | collective-permute-start | bytes 983048 | tf_op jit(solution)/shard_map/ppermute | solution.py:13
  98.3 13.1 %collective-permute-start.4 = (f32[4,5,4096]{2,1,0:T(8,128)S(1)}, f32[4,5,4096]{2,1,0:T(8,128)S(1)}, u32[]{:S(2)}, u32[]{:S(2)}) collective-permute-start(f32[4,5,4096]{2,1,0:T(8,128)S(1)} %broadcast_select_fusion), channel_id=1, source_target_pairs={{0,4},{1,5},{2,6},{3,7},{4,0},{5,1},{6,2},{7,3},{8,12},{9,13},{10,... | collective-permute-start | bytes 983048 | tf_op jit(solution)/shard_map/ppermute | solution.py:13
  114.7 12.3 %all-to-all-start.1 = ((f32[8,2,2560]{2,1,0:T(2,128)}), f32[8,2,2560]{2,1,0:T(2,128)S(1)}, u32[]{:S(2)}, u32[]{:S(2)}) async-start(f32[8,2,2560]{2,1,0:T(2,128)} %broadcast_in_dim.131), calls=%async_computation.1 | async-start | bytes 327680 | tf_op jit(solution)/shard_map/all_to_all | solution.py:29
where the time goes:
time: 129 us; the launch traced here: 128 us
  other arithmetic  47.5 us (37%)
  local copies, waits for them, and re-layouts  32.3 us (25%)
  starting transfers between devices  23.8 us (18%)
  waiting for transfers between devices  18.3 us (14%)
  between operations  4.86 us (4%)
    ppermute x6, waiting for transfers between devices, from_partner(): lax.ppermute(array, axis, [(i, i ^ 1 << stride) for i in range(lax.axis_s...  18.3 us
    select_n x3, other arithmetic, place_rows(): jnp.where(is_kept[:, None, None], fine_rows, jnp.where(is_hit[:, None, No...  14.4 us
    all_to_all x1, starting transfers between devices, sum_at_owner(): lax.all_to_all(in_blocks(array, dim, devices), axis, 0, 0, tiled=True)  10.7 us
    reduce_sum x1, other arithmetic, restrict(): jnp.mean(blocks, axis=(-5, -3, -1))  10.6 us
    select_n x2, other arithmetic, place_rows(): jnp.where(is_kept, fine_ids, jnp.where(is_hit, in_ids[place_index], -1))  7.89 us
    gather x3, local copies, waits for them, and re-layouts, take_top(): fine_rows[pick_index]  7.4 us
    select_n x1, local copies, waits for them, and re-layouts, per_device(): fine_rows = jnp.where(is_kept[:, None, None], patches, 0.0)  7.23 us
    gather x3, local copies, waits for them, and re-layouts, place_rows(): in_rows[place_index]  7.21 us
  transfers between devices with their start and end apart: 8, of which 2 were waited for; matrix products, arithmetic and copies ran while one was open for 54% of the time, Pallas kernels for 0%

commit v1 on v0

v1 whole, which is shorter than its diff:
```python
import functools

import jax
import jax.numpy as jnp
from jax import lax
from jax.experimental import pallas as pl
from jax.experimental.pallas import tpu as pltpu
from jax.sharding import PartitionSpec as P

VARS = 5
SEND = 4
TILE = 8
TILES = 3
LIVE_TILES = 2
LIVE = 12
LANES = 128
SPAN = 32
ROWS = VARS * SPAN
TILE_ROWS = ROWS * TILE
HEAD = SEND * ROWS
MSG = HEAD + 8
FINE = 20
PAR_DEV = 2
F32 = jnp.float32
I32 = jnp.int32

SMEM = pl.BlockSpec(memory_space=pltpu.SMEM)
VMEM = pl.BlockSpec(memory_space=pltpu.VMEM)
ANY = pl.BlockSpec(memory_space=pl.ANY)


def from_partner(array, mask):
    return lax.ppermute(array, "bal", [(i, i ^ mask) for i in range(8)])


def lanes():
    return lax.broadcasted_iota(I32, (8, LANES), 1)


def row_of(slot):
    return (slot // TILE) * TILE_ROWS + slot % TILE


def move(dst, dst_row, dst_step, src, src_row, src_step):
    def at(ref, row, step, chunk):
        start = row + chunk * 8 * step
        if step == 1:
            return pl.ds(pl.multiple_of(start, 8), 8)
        return pl.ds(start, 8, stride=step)

    for chunk in range(ROWS // 8):
        dst[at(dst, dst_row, dst_step, chunk), :] = src[at(src, src_row, src_step, chunk), :]


def load_kernel(live, counts, ids, x, held, msg, sems):
    copies = []
    for tile in range(LIVE_TILES):
        for var in range(VARS):
            part = pl.ds((tile * VARS + var) * SPAN * TILE, SPAN * TILE)
            copies.append(pltpu.make_async_copy(x.at[var, tile], held.at[part, :], sems.at[tile * VARS + var]))
    for copy in copies:
        copy.start()
    sent = counts[0, 0]
    first = live[0] - sent
    lane = lanes()
    head = jnp.where(lane == SEND, sent.astype(F32), 0.0)
    for lane_id in range(SEND):
        slot = jnp.minimum(first + lane_id, LIVE - 1)
        head = jnp.where(lane == lane_id, ids[slot].astype(F32), head)
    msg[pl.ds(HEAD, 8), :] = head
    for copy in copies:
        copy.wait()
    for piece in range(SEND):

        @pl.when(piece < sent)
        def _():
            move(msg, piece * ROWS, 1, held, row_of(first + piece), TILE)


def restrict_kernel(live, ids, held, parent_of, weight, out, fine, parents, sem):
    table = pltpu.make_async_copy(parent_of, parents, sem)
    table.start()
    groups = LIVE_TILES * VARS * SPAN // 8
    x = held[...].reshape(groups, 8, TILE, LANES)
    pieces = []
    for half in range(2):
        for side in range(2):
            pieces.append((x[:, half * 4 + side] + x[:, half * 4 + side + 2]).reshape(groups * TILE, LANES))
    pairs = jnp.concatenate(pieces, axis=1)
    high = pairs.astype(jnp.bfloat16)
    low = (pairs - high.astype(F32)).astype(jnp.bfloat16)
    w = weight[...]
    fine[...] = jnp.dot(high, w, preferred_element_type=F32) + jnp.dot(low, w, preferred_element_type=F32)
    out[...] = jnp.zeros_like(out)
    table.wait()
    for slot in range(LIVE):

        @pl.when(slot < live[0])
        def _():
            parent = parents[ids[slot]]
            base = (parent // PAR_DEV) * (FINE * PAR_DEV) + parent % PAR_DEV
            src = (slot // TILE) * (FINE * TILE) + slot % TILE
            for start, size in ((0, 8), (8, 8), (16, 4)):
                to = pl.ds(base + start * PAR_DEV, size, stride=PAR_DEV)
                out[to, :] += fine[pl.ds(src + start * TILE, size, stride=TILE), :]


def number(ref, lane):
    return ref[HEAD, lane].astype(I32)


def merged_ids(own, came, kept, lane):
    return jnp.where(lane < kept, own, pltpu.roll(came, kept, 1))


def pick_kernel(live, counts, ids, held, came, last, below):
    lane = lanes()
    kept = live[0] - counts[0, 0]
    held_count = kept + number(came, SEND)
    sent = counts[1, 0]
    ids_now = merged_ids(ids[...], came[pl.ds(HEAD, 8), :], kept, lane)
    for msg, first, low, high in (
        (last, held_count - sent, 0, sent),
        (below, held_count - sent - SEND, 0, SEND),
    ):
        head = pltpu.roll(ids_now, lax.rem(LANES - first, LANES), 1)
        head = jnp.where(lane == SEND, sent.astype(F32), head)
        head = jnp.where(lane == SEND + 1, counts[2, 0].astype(F32), head)
        msg[pl.ds(HEAD, 8), :] = head
        for piece in range(SEND):
            slot = first + piece
            used = jnp.logical_and(slot >= 0, piece < high)

            @pl.when(jnp.logical_and(used, slot < kept))
            def _():
                move(msg, piece * ROWS, 1, held, row_of(slot), TILE)

            @pl.when(jnp.logical_and(used, slot >= kept))
            def _():
                move(msg, piece * ROWS, 1, came, (slot - kept) * ROWS, 1)


def place_kernel(live, counts, ids, held, came, near, far, cross, out, new_ids, full, sems):
    lane = lanes()
    kept = live[0] - counts[0, 0]
    c0 = number(came, SEND)
    c1, c2 = counts[1, 0], counts[2, 0]
    n1 = number(near, SEND)
    f2 = number(far, SEND + 1)
    x1 = number(cross, SEND)
    own = kept + c0 - c1 - jnp.maximum(c2 - n1, 0)
    from_near = jnp.maximum(n1 - c2, 0)
    from_far = jnp.maximum(f2 - x1, 0)
    from_cross = jnp.minimum(x1, f2)
    bare = jnp.minimum(own, kept)

    sub = lax.broadcasted_iota(I32, (TILE, LANES), 0)
    for tile in range(TILES):
        rows = pl.ds(tile * TILE_ROWS, TILE_ROWS)
        if tile < LIVE_TILES:
            keep = (sub + tile * TILE < bare)[None]
            part = held[rows, :].reshape(ROWS, TILE, LANES)
            full[rows, :] = jnp.where(keep, part, 0.0).reshape(TILE_ROWS, LANES)
        else:
            full[rows, :] = jnp.zeros((TILE_ROWS, LANES), F32)

    marks = ids[...]
    at = kept
    new = jnp.where(lane < bare, marks, -1.0)
    start = bare
    for msg, skip, amount in (
        (came, 0, own - bare),
        (near, 0, from_near),
        (far, SEND - from_far, from_far),
        (cross, x1 - from_cross, from_cross),
    ):
        shift = lax.rem(start - skip + LANES, LANES)
        moved = pltpu.roll(msg[pl.ds(HEAD, 8), :], shift, 1)
        inside = jnp.logical_and(lane >= start, lane < start + amount)
        new = jnp.where(inside, moved, new)
        for piece in range(SEND):

            @pl.when(piece < amount)
            def _(msg=msg, piece=piece, start=start, skip=skip):
                move(full, row_of(start + piece), TILE, msg, (skip + piece) * ROWS, 1)

        start = start + amount
    new_ids[...] = new.astype(I32)
    copies = []
    for tile in range(TILES):
        for var in range(VARS):
            part = pl.ds((tile * VARS + var) * SPAN * TILE, SPAN * TILE)
            copies.append(pltpu.make_async_copy(full.at[part, :], out.at[var, tile], sems.at[tile * VARS + var]))
    for copy in copies:
        copy.start()
    for copy in copies:
        copy.wait()


def restriction_weight():
    lane = jnp.arange(LANES)
    column = ((lane // 32) * 8 + (lane % 16) // 2)[:, None]
    target = jnp.arange(LANES)[None, :]
    return jnp.concatenate(
        [jnp.where(target == group * 32 + column, 0.125, 0.0) for group in range(4)], axis=0
    ).astype(jnp.bfloat16)


def call(kernel, outs, ins, out_specs, scratch=(), **kw):
    return pl.pallas_call(
        kernel, out_shape=outs, in_specs=ins, out_specs=out_specs, scratch_shapes=list(scratch), **kw
    )


def per_device(patches, patch_ids, live, counts, parent_of):
    slots = patches.shape[0]
    levels = lax.axis_size("level")
    x = patches.transpose(1, 0, 2).reshape(VARS, TILES, TILE, SPAN, LANES)
    x = x.transpose(0, 1, 3, 2, 4).reshape(VARS, TILES, SPAN * TILE, LANES)
    marks = jnp.broadcast_to(jnp.pad(patch_ids.astype(F32), (0, LANES - slots))[None], (8, LANES))
    message = jax.ShapeDtypeStruct((MSG, LANES), F32)
    held, first = call(
        load_kernel,
        (jax.ShapeDtypeStruct((LIVE_TILES * TILE_ROWS, LANES), F32), message),
        [SMEM, SMEM, SMEM, ANY],
        (VMEM, VMEM),
        [pltpu.SemaphoreType.DMA((LIVE_TILES * VARS,))],
        name="load",
    )(live, counts, patch_ids, x)
    came = from_partner(first, 1)
    block = FINE * PAR_DEV
    partial = call(
        restrict_kernel,
        jax.ShapeDtypeStruct((levels * block, LANES), F32),
        [SMEM, SMEM, VMEM, ANY, VMEM],
        VMEM,
        [
            pltpu.VMEM((LIVE_TILES * TILE * FINE, LANES), F32),
            pltpu.SMEM(parent_of.shape, I32),
            pltpu.SemaphoreType.DMA,
        ],
        name="restrict",
    )(live, patch_ids, held, parent_of, restriction_weight())
    last, below = call(
        pick_kernel, (message, message), [SMEM, SMEM, VMEM, VMEM, VMEM], (VMEM, VMEM), name="pick"
    )(live, counts, marks, held, came)
    far = from_partner(below, 4)
    near = from_partner(last, 2)
    cross = from_partner(last, 6)

    tiles = lax.all_to_all(partial.reshape(levels, block, LANES), "level", 0, 0, tiled=True)
    sums = jnp.sum(tiles, axis=0)
    sums = sums + from_partner(sums, 2) + from_partner(sums, 6) + from_partner(sums, 4)
    sums = sums + from_partner(sums, 1)
    coarse = sums.reshape(VARS, FINE // VARS, PAR_DEV, LANES).transpose(2, 0, 1, 3).reshape(PAR_DEV, VARS, -1)

    out, new_ids = call(
        place_kernel,
        (jax.ShapeDtypeStruct((VARS, TILES, SPAN * TILE, LANES), F32), jax.ShapeDtypeStruct((8, LANES), I32)),
        [SMEM, SMEM, VMEM, VMEM, VMEM, VMEM, VMEM, VMEM],
        (ANY, VMEM),
        [pltpu.VMEM((TILES * TILE_ROWS, LANES), F32), pltpu.SemaphoreType.DMA((TILES * VARS,))],
        name="place",
    )(live, counts, marks, held, came, near, far, cross)
    out = out.reshape(VARS, TILES, SPAN, TILE, LANES).transpose(0, 1, 3, 2, 4)
    out = out.reshape(VARS, slots, SPAN * LANES).transpose(1, 0, 2)
    return (out, new_ids[0, :slots], coarse)


def solution(mesh):
    return jax.shard_map(
        per_device,
        mesh=mesh,
        in_specs=(
            P(("level", "bal"), None, None),
            P(("level", "bal")),
            P(("level", "bal")),
            P(None, ("level", "bal")),
            P(),
        ),
        out_specs=(P(("level", "bal"), None, None), P(("level", "bal")), P("level", None, None)),
        check_vma=False,
    )
```

time: 129 us -> 58.6 us (0.45)
  other arithmetic: 47.5 us -> 1.58 us
  local copies, waits for them, and re-layouts: 32.3 us -> 3.97 us
  Pallas kernels: 0 us -> 13.7 us
  waiting for transfers between devices: 18.3 us -> 14.7 us
  between operations: 4.86 us -> 1.42 us
    select_n x17 -> x0, other arithmetic: 30.7 us -> none  [the longest x3 14.4 us: place_rows(): jnp.where(is_kept[:, None, None], fine_rows, jnp.where(is_hit[:, None, No...]
    gather x13 -> x0, local copies, waits for them, and re-layouts: 19.2 us -> none  [the longest x3 7.4 us: take_top(): fine_rows[pick_index]]
    pallas_call x0 -> x4, Pallas kernels: none -> 13.7 us  [the longest x1 4.17 us: per_device(): call(place_kernel, (jax.ShapeDtypeStruct((VARS, TILES, SPAN * TILE, LANES...]
    ppermute x6 -> x8, waiting for transfers between devices: 18.3 us -> 5.56 us  [from_partner(): return lax.ppermute(array, 'bal', [(i, i ^ mask) for i in range(8)])]
    reduce_sum x5 -> x1, other arithmetic: 12.7 us -> 0.05 us  [per_device(): sums = jnp.sum(tiles, axis=0)]
    all_to_all x2 -> x1, waiting for transfers between devices: 0.01 us -> 9.14 us  [per_device(): lax.all_to_all(partial.reshape(levels, block, LANES), 'level', 0, 0, tile...]
    select_n x1 -> x0, local copies, waits for them, and re-layouts: 7.23 us -> none  [per_device(): fine_rows = jnp.where(is_kept[:, None, None], patches, 0.0)]
    all_to_all x2 -> x1, starting transfers between devices: 17 us -> 12 us  [per_device(): lax.all_to_all(partial.reshape(levels, block, LANES), 'level', 0, 0, tile...]
  transfers between devices with their start and end apart: 8 -> 9, of which waited for: 2 -> 4; matrix products, arithmetic and copies ran while one was open for 54% -> 3% of each run, Pallas kernels for 0% -> 12%
where the time goes in v1:
time: 58.6 us; the launch traced here: 58.1 us
  starting transfers between devices  22.7 us (39%)
  waiting for transfers between devices  14.7 us (25%)
  Pallas kernels  13.7 us (23%)
  local copies, waits for them, and re-layouts  3.97 us (7%)
  other arithmetic  1.58 us (3%)
  between operations  1.42 us (2%)
    all_to_all x1, starting transfers between devices, per_device(): lax.all_to_all(partial.reshape(levels, block, LANES), 'level', 0, 0, tile...  12 us
    ppermute x8, starting transfers between devices, from_partner(): return lax.ppermute(array, 'bal', [(i, i ^ mask) for i in range(8)])  10.7 us
    all_to_all x1, waiting for transfers between devices, per_device(): lax.all_to_all(partial.reshape(levels, block, LANES), 'level', 0, 0, tile...  9.14 us
    ppermute x8, waiting for transfers between devices, from_partner(): return lax.ppermute(array, 'bal', [(i, i ^ mask) for i in range(8)])  5.56 us
    pallas_call x1, Pallas kernels, per_device(): call(place_kernel, (jax.ShapeDtypeStruct((VARS, TILES, SPAN * TILE, LANES...  4.17 us
    pallas_call x1, Pallas kernels, per_device(): call(restrict_kernel, jax.ShapeDtypeStruct((levels * block, LANES), F32),...  3.47 us
    pallas_call x1, Pallas kernels, per_device(): call(load_kernel, (jax.ShapeDtypeStruct((LIVE_TILES * TILE_ROWS, LANES),...  3.42 us
    pallas_call x1, Pallas kernels, per_device(): call(pick_kernel, (message, message), [SMEM, SMEM, VMEM, VMEM, VMEM], (VM...  2.66 us
  transfers between devices with their start and end apart: 9, of which 4 were waited for; matrix products, arithmetic and copies ran while one was open for 3% of the time, Pallas kernels for 12%

profile of v1, /device:TPU:1, one launch (start us, length us, event | category | flops | bytes accessed | tf_op | source)
XLA Modules:
  0.0 58.1 jit_solution(534309170691909128)
XLA Ops:
  1.3 1.3 %copy.13.counts = s32[3,1]{1,0:T(4,128)} copy(s32[3,1]{0,1:T(1,128)} %param.8) | data formatting | bytes 24 | tf_op args[3]
  2.7 0.1 select_convert_fusion
  2.8 0.1 select_convert_fusion.2
  2.9 3.4 %load.1 = (f32[2560,128]{1,0:T(8,128)}, f32[648,128]{1,0:T(8,128)}) custom-call(s32[1]{0:T(128)S(6)} %copy.14.live, s32[3,1]{1,0:T(4,128)} %copy.13.counts, s32[24]{0:T(128)} %ids.3, f32[5,3,256,128]{3,2,1,0:T(8,128)} %bitcast.23), custom_call_target="tpu_custom_call" | custom-call | tf_op jit(solution)/shard_map/load/pallas_call | solution.py:222
  6.3 0.0 copy-start.5
  6.3 0.0 copy-start.4
  6.3 0.7 %pad_maximum_fusion.weight = bf16[512,128]{1,0:T(8,128)(2,1)} fusion(bf16[128,128]{1,0:T(8,128)(2,1)S(1)} %get-tuple-element.15, bf16[128,128]{1,0:T(8,128)(2,1)S(1)} %get-tuple-element.16, bf16[128,128]{1,0:T(8,128)(2,1)S(1)} %get-tuple-element.17, bf16[128,128]{1,0:T(8,128)(2,1)S(1)} %get-tuple-element.18), kind=kLoop, calls=%fused_computation | loop fusion | flops 524288 | bytes 262144 | tf_op jit(solution)/shard_map/concatenate | solution.py:204
  7.0 3.5 %restrict.1 = f32[1280,128]{1,0:T(8,128)} custom-call(s32[1]{0:T(128)S(6)} %copy.14.live, s32[24]{0:T(128)} %ids.3, f32[2560,128]{1,0:T(8,128)} %get-tuple-element.9.held, s32[6144]{0:T(1024)} %parent_of.1, bf16[512,128]{1,0:T(8,128)(2,1)} %pad_maximum_fusion.weight), custom_call_target="tpu_custom_call" | custom-call | tf_op jit(solution)/shard_map/restrict/pallas_call | solution.py:232
  10.5 12.0 %all-to-all-start = ((f32[32,40,128]{2,1,0:T(8,128)}), f32[32,40,128]{2,1,0:T(8,128)S(1)}, u32[]{:S(2)}, u32[]{:S(2)}) async-start(f32[32,40,128]{2,1,0:T(8,128)} %bitcast.22), calls=%async_computation | async-start | bytes 1310720 | tf_op jit(solution)/shard_map/all_to_all | solution.py:251
  22.5 0.0 copy-done.5
  22.5 1.0 %collective-permute-start = (f32[648,128]{1,0:T(8,128)S(1)}, f32[648,128]{1,0:T(8,128)S(1)}, u32[]{:S(2)}, u32[]{:S(2)}) collective-permute-start(f32[648,128]{1,0:T(8,128)S(1)} %copy-done.5), channel_id=1, source_target_pairs={{0,1},{1,0},{2,3},{3,2},{4,5},{5,4},{6,7},{7,6},{8,9},{9,8},{10,11... | collective-permute-start | bytes 995336 | tf_op jit(solution)/shard_map/ppermute | solution.py:33
  23.5 0.0 copy-done.4
  23.5 1.2 %collective-permute-done.came = f32[648,128]{1,0:T(8,128)S(1)} collective-permute-done((f32[648,128]{1,0:T(8,128)S(1)}, f32[648,128]{1,0:T(8,128)S(1)}, u32[]{:S(2)}, u32[]{:S(2)}) %collective-permute-start) | collective-permute-done | bytes 331808 | tf_op jit(solution)/shard_map/ppermute | solution.py:33
  24.7 0.0 copy-start
  24.7 0.6 %broadcast_in_dim.22.ids = f32[8,128]{1,0:T(8,128)} broadcast(f32[128]{0:T(128)S(1)} %pad.4), dimensions={1} | broadcast | bytes 4608 | tf_op jit(solution)/shard_map/broadcast_in_dim | solution.py:220
  25.3 0.1 copy-done
  25.4 2.7 %pick.1 = (f32[648,128]{1,0:T(8,128)}, f32[648,128]{1,0:T(8,128)}) custom-call(s32[1]{0:T(128)S(6)} %copy.14.live, s32[3,1]{1,0:T(4,128)} %copy.13.counts, f32[8,128]{1,0:T(8,128)} %broadcast_in_dim.22.ids, f32[2560,128]{1,0:T(8,128)} %get-tuple-element.9.held, f32[648,128]{1,0:T(8,128)} %copy-done), custom_call_target="tpu_custom_call" | custom-call | tf_op jit(solution)/shard_map/pick/pallas_call | solution.py:244
  28.1 1.3 %collective-permute-start.1 = (f32[648,128]{1,0:T(8,128)}, f32[648,128]{1,0:T(8,128)S(1)}, u32[]{:S(2)}, u32[]{:S(2)}) collective-permute-start(f32[648,128]{1,0:T(8,128)} %get-tuple-element.11), channel_id=1, source_target_pairs={{0,2},{1,3},{2,0},{3,1},{4,6},{5,7},{6,4},{7,5},{8,10},{9,11},{10,... | collective-permute-start | bytes 995336 | tf_op jit(solution)/shard_map/ppermute | solution.py:33
  29.4 2.5 %collective-permute-start.2 = (f32[648,128]{1,0:T(8,128)}, f32[648,128]{1,0:T(8,128)S(1)}, u32[]{:S(2)}, u32[]{:S(2)}) collective-permute-start(f32[648,128]{1,0:T(8,128)} %get-tuple-element.12), channel_id=1, source_target_pairs={{0,4},{1,5},{2,6},{3,7},{4,0},{5,1},{6,2},{7,3},{8,12},{9,13},{10,... | collective-permute-start | bytes 995336 | tf_op jit(solution)/shard_map/ppermute | solution.py:33
  31.8 0.1 collective-permute-start.3
  32.0 9.1 %all-to-all-done = f32[32,40,128]{2,1,0:T(8,128)S(1)} async-done(((f32[32,40,128]{2,1,0:T(8,128)}), f32[32,40,128]{2,1,0:T(8,128)S(1)}, u32[]{:S(2)}, u32[]{:S(2)}) %all-to-all-start) | async-done | bytes 655392 | tf_op jit(solution)/shard_map/all_to_all | solution.py:251
  41.1 0.1 reduce_sum.9
  41.2 2.8 %collective-permute-start.6 = (f32[40,128]{1,0:T(8,128)S(1)}, f32[40,128]{1,0:T(8,128)S(1)}, u32[]{:S(2)}, u32[]{:S(2)}) collective-permute-start(f32[40,128]{1,0:T(8,128)S(1)} %reduce_sum.9), channel_id=1, source_target_pairs={{0,4},{1,5},{2,6},{3,7},{4,0},{5,1},{6,2},{7,3},{8,12},{9,13},{10,... | collective-permute-start | bytes 61448 | tf_op jit(solution)/shard_map/ppermute | solution.py:33
  44.0 0.9 %collective-permute-start.5 = (f32[40,128]{1,0:T(8,128)S(1)}, f32[40,128]{1,0:T(8,128)S(1)}, u32[]{:S(2)}, u32[]{:S(2)}) collective-permute-start(f32[40,128]{1,0:T(8,128)S(1)} %reduce_sum.9), channel_id=1, source_target_pairs={{0,6},{1,7},{2,4},{3,5},{4,2},{5,3},{6,0},{7,1},{8,14},{9,15},{10,... | collective-permute-start | bytes 61448 | tf_op jit(solution)/shard_map/ppermute | solution.py:33
  44.9 0.0 collective-permute-done.1.near
  44.9 0.0 copy-start.1
  44.9 0.0 collective-permute-start.4
  44.9 1.8 %collective-permute-done.2.far = f32[648,128]{1,0:T(8,128)S(1)} collective-permute-done((f32[648,128]{1,0:T(8,128)}, f32[648,128]{1,0:T(8,128)S(1)}, u32[]{:S(2)}, u32[]{:S(2)}) %collective-permute-start.2) | collective-permute-done | bytes 331808 | tf_op jit(solution)/shard_map/ppermute | solution.py:33
  46.7 0.0 copy-start.2
  46.7 2.5 %collective-permute-done.3.cross = f32[648,128]{1,0:T(8,128)S(1)} collective-permute-done((f32[648,128]{1,0:T(8,128)}, f32[648,128]{1,0:T(8,128)S(1)}, u32[]{:S(2)}, u32[]{:S(2)}) %collective-permute-start.3) | collective-permute-done | bytes 331808 | tf_op jit(solution)/shard_map/ppermute | solution.py:33
  49.2 0.0 copy-done.1
  49.2 0.0 copy-done.2
  49.2 0.0 copy-start.3
  49.2 0.7 %copy-done.3 = f32[648,128]{1,0:T(8,128)} copy-done((f32[648,128]{1,0:T(8,128)}, f32[648,128]{1,0:T(8,128)S(1)}, u32[]{:S(2)}) %copy-start.3) | copy-done | bytes 331800
  50.0 4.2 %place.1 = (f32[5,3,256,128]{3,2,1,0:T(8,128)}, s32[8,128]{1,0:T(8,128)}) custom-call(s32[1]{0:T(128)S(6)} %copy.14.live, s32[3,1]{1,0:T(4,128)} %copy.13.counts, f32[8,128]{1,0:T(8,128)} %broadcast_in_dim.22.ids, f32[2560,128]{1,0:T(8,128)} %get-tuple-element.9.held, f32[648,128]{1,0:T(8,128)} %copy-done, f32[648,128]{1,0:T(8,128)} %copy-done.1, ...), custom_call_target="tpu_custom_call" | custom-call | tf_op jit(solution)/shard_map/place/pallas_call | solution.py:257
  54.1 0.0 collective-permute-done.6
  54.1 0.0 collective-permute-done.5
  54.2 0.0 collective-permute-done.4
  54.2 2.1 %collective-permute-start.7 = (f32[40,128]{1,0:T(8,128)S(1)}, f32[40,128]{1,0:T(8,128)S(1)}, u32[]{:S(2)}, u32[]{:S(2)}) collective-permute-start(f32[40,128]{1,0:T(8,128)S(1)} %add_add_fusion), channel_id=1, source_target_pairs={{0,1},{1,0},{2,3},{3,2},{4,5},{5,4},{6,7},{7,6},{8,9},{9,8},{10,11... | collective-permute-start | bytes 61448 | tf_op jit(solution)/shard_map/ppermute | solution.py:33
  56.3 1.2 %slice_bitcast_fusion = s32[24]{0:T(128)} fusion(s32[8,128]{1,0:T(8,128)} %get-tuple-element.14), kind=kLoop, calls=%fused_computation.22 | loop fusion | bytes 192 | tf_op jit(solution)/shard_map/squeeze | solution.py:267
  57.5 0.0 collective-permute-done.7
  57.5 0.6 %add.133 = f32[40,128]{1,0:T(8,128)} add(f32[40,128]{1,0:T(8,128)S(1)} %add_add_fusion, f32[40,128]{1,0:T(8,128)S(1)} %collective-permute-done.7) | non-fusion elementwise | flops 5120 | bytes 61440 | tf_op jit(solution)/shard_map/add | solution.py:254
  (7 shorter events, 0.1 us)
Async XLA Ops:
  6.3 16.2 %copy-start.5 = (f32[648,128]{1,0:T(8,128)S(1)}, f32[648,128]{1,0:T(8,128)}, u32[]{:S(2)}) copy-start(f32[648,128]{1,0:T(8,128)} %get-tuple-element.10) | copy-start | bytes 995332
  6.3 17.2 %copy-start.4 = (s32[24]{0:T(128)S(1)}, s32[24]{0:T(128)}, u32[]{:S(2)}) copy-start(s32[24]{0:T(128)} %ids.3) | copy-start | bytes 292
  10.5 30.6 %all-to-all-start = ((f32[32,40,128]{2,1,0:T(8,128)}), f32[32,40,128]{2,1,0:T(8,128)S(1)}, u32[]{:S(2)}, u32[]{:S(2)}) async-start(f32[32,40,128]{2,1,0:T(8,128)} %bitcast.22), calls=%async_computation | async-start | bytes 1310720 | tf_op jit(solution)/shard_map/all_to_all | solution.py:251
  22.5 2.2 %collective-permute-start = (f32[648,128]{1,0:T(8,128)S(1)}, f32[648,128]{1,0:T(8,128)S(1)}, u32[]{:S(2)}, u32[]{:S(2)}) collective-permute-start(f32[648,128]{1,0:T(8,128)S(1)} %copy-done.5), channel_id=1, source_target_pairs={{0,1},{1,0},{2,3},{3,2},{4,5},{5,4},{6,7},{7,6},{8,9},{9,8},{10,11... | collective-permute-start | bytes 995336 | tf_op jit(solution)/shard_map/ppermute | solution.py:33
  24.7 0.7 %copy-start = (f32[648,128]{1,0:T(8,128)}, f32[648,128]{1,0:T(8,128)S(1)}, u32[]{:S(2)}) copy-start(f32[648,128]{1,0:T(8,128)S(1)} %collective-permute-done.came) | copy-start | bytes 995332
  28.1 16.8 %collective-permute-start.1 = (f32[648,128]{1,0:T(8,128)}, f32[648,128]{1,0:T(8,128)S(1)}, u32[]{:S(2)}, u32[]{:S(2)}) collective-permute-start(f32[648,128]{1,0:T(8,128)} %get-tuple-element.11), channel_id=1, source_target_pairs={{0,2},{1,3},{2,0},{3,1},{4,6},{5,7},{6,4},{7,5},{8,10},{9,11},{10,... | collective-permute-start | bytes 995336 | tf_op jit(solution)/shard_map/ppermute | solution.py:33
  29.4 17.3 %collective-permute-start.2 = (f32[648,128]{1,0:T(8,128)}, f32[648,128]{1,0:T(8,128)S(1)}, u32[]{:S(2)}, u32[]{:S(2)}) collective-permute-start(f32[648,128]{1,0:T(8,128)} %get-tuple-element.12), channel_id=1, source_target_pairs={{0,4},{1,5},{2,6},{3,7},{4,0},{5,1},{6,2},{7,3},{8,12},{9,13},{10,... | collective-permute-start | bytes 995336 | tf_op jit(solution)/shard_map/ppermute | solution.py:33
  31.8 17.4 %collective-permute-start.3 = (f32[648,128]{1,0:T(8,128)}, f32[648,128]{1,0:T(8,128)S(1)}, u32[]{:S(2)}, u32[]{:S(2)}) collective-permute-start(f32[648,128]{1,0:T(8,128)} %get-tuple-element.11), channel_id=1, source_target_pairs={{0,6},{1,7},{2,4},{3,5},{4,2},{5,3},{6,0},{7,1},{8,14},{9,15},{10,... | collective-permute-start | bytes 995336 | tf_op jit(solution)/shard_map/ppermute | solution.py:33
  41.2 13.0 %collective-permute-start.6 = (f32[40,128]{1,0:T(8,128)S(1)}, f32[40,128]{1,0:T(8,128)S(1)}, u32[]{:S(2)}, u32[]{:S(2)}) collective-permute-start(f32[40,128]{1,0:T(8,128)S(1)} %reduce_sum.9), channel_id=1, source_target_pairs={{0,4},{1,5},{2,6},{3,7},{4,0},{5,1},{6,2},{7,3},{8,12},{9,13},{10,... | collective-permute-start | bytes 61448 | tf_op jit(solution)/shard_map/ppermute | solution.py:33
  44.0 10.2 %collective-permute-start.5 = (f32[40,128]{1,0:T(8,128)S(1)}, f32[40,128]{1,0:T(8,128)S(1)}, u32[]{:S(2)}, u32[]{:S(2)}) collective-permute-start(f32[40,128]{1,0:T(8,128)S(1)} %reduce_sum.9), channel_id=1, source_target_pairs={{0,6},{1,7},{2,4},{3,5},{4,2},{5,3},{6,0},{7,1},{8,14},{9,15},{10,... | collective-permute-start | bytes 61448 | tf_op jit(solution)/shard_map/ppermute | solution.py:33
  44.9 4.3 %copy-start.1 = (f32[648,128]{1,0:T(8,128)}, f32[648,128]{1,0:T(8,128)S(1)}, u32[]{:S(2)}) copy-start(f32[648,128]{1,0:T(8,128)S(1)} %collective-permute-done.1.near) | copy-start | bytes 995332
  44.9 9.2 %collective-permute-start.4 = (f32[40,128]{1,0:T(8,128)S(1)}, f32[40,128]{1,0:T(8,128)S(1)}, u32[]{:S(2)}, u32[]{:S(2)}) collective-permute-start(f32[40,128]{1,0:T(8,128)S(1)} %reduce_sum.9), channel_id=1, source_target_pairs={{0,2},{1,3},{2,0},{3,1},{4,6},{5,7},{6,4},{7,5},{8,10},{9,11},{10,... | collective-permute-start | bytes 61448 | tf_op jit(solution)/shard_map/ppermute | solution.py:33
  46.7 2.5 %copy-start.2 = (f32[648,128]{1,0:T(8,128)}, f32[648,128]{1,0:T(8,128)S(1)}, u32[]{:S(2)}) copy-start(f32[648,128]{1,0:T(8,128)S(1)} %collective-permute-done.2.far) | copy-start | bytes 995332
  49.2 0.7 %copy-start.3 = (f32[648,128]{1,0:T(8,128)}, f32[648,128]{1,0:T(8,128)S(1)}, u32[]{:S(2)}) copy-start(f32[648,128]{1,0:T(8,128)S(1)} %collective-permute-done.3.cross) | copy-start | bytes 995332
  54.2 3.3 %collective-permute-start.7 = (f32[40,128]{1,0:T(8,128)S(1)}, f32[40,128]{1,0:T(8,128)S(1)}, u32[]{:S(2)}, u32[]{:S(2)}) collective-permute-start(f32[40,128]{1,0:T(8,128)S(1)} %add_add_fusion), channel_id=1, source_target_pairs={{0,1},{1,0},{2,3},{3,2},{4,5},{5,4},{6,7},{7,6},{8,9},{9,8},{10,11... | collective-permute-start | bytes 61448 | tf_op jit(solution)/shard_map/ppermute | solution.py:33

commit v2 on v1

v2 whole, which is shorter than its diff:
```python
import jax
import jax.numpy as jnp
from jax import lax
from jax.experimental import pallas as pl
from jax.experimental.pallas import tpu as pltpu
from jax.sharding import PartitionSpec as P


VARS = 5
SEND = 4
TILE = 8
TILES = 3
LIVE_TILES = 2
LIVE = 12
LANES = 128
SPAN = 32
ROWS = VARS * SPAN
TILE_ROWS = ROWS * TILE
HEAD = SEND * ROWS
MSG = HEAD + 8
FINE = 20
PAR_DEV = 2
NEAR_LEVELS = 4
FAR_LEVELS = 8
PIECE = FAR_LEVELS * FINE
F32 = jnp.float32
I32 = jnp.int32
LIVE_AT = 16
COUNTS_AT = 17
PARENTS_AT = 32

SMEM = pl.BlockSpec(memory_space=pltpu.SMEM)
VMEM = pl.BlockSpec(memory_space=pltpu.VMEM)
HBM = pl.BlockSpec(memory_space=pltpu.HBM)


def from_partner(array, axis, mask):
    return lax.ppermute(array, axis, [(i, i ^ mask) for i in range(lax.axis_size(axis))])


def lanes():
    return lax.broadcasted_iota(I32, (8, LANES), 1)


def row_of(slot):
    return (slot // TILE) * TILE_ROWS + slot % TILE


def fill_weight(weight):
    lane = lax.broadcasted_iota(I32, (LANES, LANES), 0)
    target = lax.broadcasted_iota(I32, (LANES, LANES), 1)
    column = (lane // 32) * 8 + (lane % 16) // 2
    for group in range(4):
        part = jnp.where(target == group * 32 + column, 0.125, 0.0)
        weight[pl.ds(group * LANES, LANES), :] = part.astype(jnp.bfloat16)


def rows_at(row, step, chunk):
    start = row + chunk * 8 * step
    if step == 1:
        return pl.ds(pl.multiple_of(start, 8), 8)
    return pl.ds(start, 8, stride=step)


def move(dst, dst_row, dst_step, src, src_row, src_step, chunks=range(ROWS // 8)):
    for chunk in chunks:
        dst[rows_at(dst_row, dst_step, chunk), :] = src[rows_at(src_row, src_step, chunk), :]


def block_copies(hbm, vmem, sems, tiles, var, inward):
    copies = []
    for tile in tiles:
        part = vmem.at[pl.ds((tile * VARS + var) * SPAN * TILE, SPAN * TILE), :]
        ends = (hbm.at[var, tile], part) if inward else (part, hbm.at[var, tile])
        copies.append(pltpu.make_async_copy(*ends, sems.at[tile * VARS + var]))
    return copies


def load_kernel(
    live, counts, ids, parent_of, x, held, msg, weight, info, counts_s, ids_s, parents, sems, small_sems
):
    small = [
        pltpu.make_async_copy(src, dst, small_sems.at[i])
        for i, (src, dst) in enumerate(((counts, counts_s), (ids, ids_s), (parent_of, parents)))
    ]
    for copy in small:
        copy.start()
    copies = []
    for var in range(VARS):
        copies += block_copies(x, held, sems, range(LIVE_TILES), var, True)
    for copy in copies:
        copy.start()
    fill_weight(weight)
    for copy in small:
        copy.wait()
    sent = counts_s[0]
    first = live[0] - sent
    lane = lanes()
    head = jnp.where(lane == SEND, sent.astype(F32), 0.0)
    for lane_id in range(SEND):
        slot = jnp.minimum(first + lane_id, LIVE - 1)
        head = jnp.where(lane == lane_id, ids_s[slot].astype(F32), head)
    msg[pl.ds(HEAD, 8), :] = head
    numbers = jnp.where(lane == LIVE_AT, live[0], 0)
    for turn in range(3):
        numbers = jnp.where(lane == COUNTS_AT + turn, counts_s[turn], numbers)
    for slot in range(LIVE):
        mark = ids_s[slot]
        numbers = jnp.where(lane == slot, mark, numbers)
        numbers = jnp.where(lane == PARENTS_AT + slot, parents[mark], numbers)
    info[...] = numbers
    for copy in copies:
        copy.wait()
    for piece in range(SEND):

        @pl.when(piece < sent)
        def _(piece=piece):
            move(msg, piece * ROWS, 1, held, row_of(first + piece), TILE)


def restrict_kernel(info, held, weight, mine, other, fine):
    groups = LIVE_TILES * VARS * SPAN // 8
    x = held[...].reshape(groups, 8, TILE, LANES)
    pieces = []
    for half in range(2):
        for side in range(2):
            pieces.append((x[:, half * 4 + side] + x[:, half * 4 + side + 2]).reshape(groups * TILE, LANES))
    pairs = jnp.concatenate(pieces, axis=1)
    high = pairs.astype(jnp.bfloat16)
    low = (pairs - high.astype(F32)).astype(jnp.bfloat16)
    w = weight[...]
    fine[...] = jnp.dot(high, w, preferred_element_type=F32) + jnp.dot(low, w, preferred_element_type=F32)
    mine[...] = jnp.zeros_like(mine)
    other[...] = jnp.zeros_like(other)
    core = lax.axis_index("bal") % PAR_DEV
    place = lax.axis_index("level") % NEAR_LEVELS
    live = info[0, LIVE_AT]
    for slot in range(LIVE):
        parent = info[0, PARENTS_AT + slot]
        level = parent // PAR_DEV
        near = jnp.bitwise_xor(level % NEAR_LEVELS, place)
        base = near * PIECE + (level // NEAR_LEVELS) * FINE
        src = (slot // TILE) * (FINE * TILE) + slot % TILE
        here = parent % PAR_DEV == core
        for out, wanted in ((mine, here), (other, jnp.logical_not(here))):

            @pl.when(jnp.logical_and(slot < live, wanted))
            def _(out=out, base=base, src=src):
                for start, size in ((0, 8), (8, 8), (16, 4)):
                    out[pl.ds(base + start, size), :] += fine[pl.ds(src + start * TILE, size, stride=TILE), :]


def add_kernel(mine, other, *outs):
    for near, out in enumerate(outs):
        rows = pl.ds(near * PIECE, PIECE)
        out[...] = mine[rows, :] + other[rows, :]


def number(ref, lane):
    return ref[HEAD, lane].astype(I32)


def head_of(ref):
    return ref[pl.ds(HEAD, 8), :]


def pick_kernel(info, held, came, last, below):
    lane = lanes()
    sent = info[0, COUNTS_AT + 1]
    kept = info[0, LIVE_AT] - info[0, COUNTS_AT]
    held_count = kept + number(came, SEND)
    marks = info[...].astype(F32)
    marks = jnp.where(lane < kept, marks, pltpu.roll(head_of(came), kept, 1))
    for msg, first, pieces in ((last, held_count - sent, sent), (below, held_count - sent - SEND, SEND)):
        head = pltpu.roll(marks, lax.rem(LANES - first, LANES), 1)
        head = jnp.where(lane == SEND, sent.astype(F32), head)
        head = jnp.where(lane == SEND + 1, info[0, COUNTS_AT + 2].astype(F32), head)
        msg[pl.ds(HEAD, 8), :] = head
        for piece in range(SEND):
            slot = first + piece
            used = jnp.logical_and(slot >= 0, piece < pieces)

            @pl.when(jnp.logical_and(used, slot < kept))
            def _(msg=msg, piece=piece, slot=slot):
                move(msg, piece * ROWS, 1, held, row_of(slot), TILE)

            @pl.when(jnp.logical_and(used, slot >= kept))
            def _(msg=msg, piece=piece, slot=slot):
                move(msg, piece * ROWS, 1, came, (slot - kept) * ROWS, 1)


def place_kernel(info, x, came, near, far, cross, out, new_ids, full, in_sems, out_sems):
    loads = []
    for var in range(VARS):
        loads.append(block_copies(x, full, in_sems, range(LIVE_TILES), var, True))
    for copies in loads:
        for copy in copies:
            copy.start()
    lane = lanes()
    kept = info[0, LIVE_AT] - info[0, COUNTS_AT]
    c0 = number(came, SEND)
    c1, c2 = info[0, COUNTS_AT + 1], info[0, COUNTS_AT + 2]
    n1 = number(near, SEND)
    f2 = number(far, SEND + 1)
    x1 = number(cross, SEND)
    own = kept + c0 - c1 - jnp.maximum(c2 - n1, 0)
    from_near = jnp.maximum(n1 - c2, 0)
    from_far = jnp.maximum(f2 - x1, 0)
    from_cross = jnp.minimum(x1, f2)
    bare = jnp.minimum(own, kept)

    new = jnp.where(lane < bare, info[...].astype(F32), -1.0)
    start = bare
    parts = []
    for msg, skip, amount in (
        (came, 0, own - bare),
        (near, 0, from_near),
        (far, SEND - from_far, from_far),
        (cross, x1 - from_cross, from_cross),
    ):
        moved = pltpu.roll(head_of(msg), lax.rem(start - skip + LANES, LANES), 1)
        new = jnp.where(jnp.logical_and(lane >= start, lane < start + amount), moved, new)
        parts.append((msg, skip, amount, start))
        start = start + amount
    new_ids[...] = new[0:1, : TILE * TILES].astype(I32)

    sub = lax.broadcasted_iota(I32, (TILE, LANES), 0)
    stores = []
    for var in range(VARS):
        for copy in loads[var]:
            copy.wait()
        for tile in range(TILES):
            rows = pl.ds((tile * VARS + var) * SPAN * TILE, SPAN * TILE)
            if tile < LIVE_TILES:
                keep = (sub + tile * TILE < bare)[None]
                part = full[rows, :].reshape(SPAN, TILE, LANES)
                full[rows, :] = jnp.where(keep, part, 0.0).reshape(SPAN * TILE, LANES)
            else:
                full[rows, :] = jnp.zeros((SPAN * TILE, LANES), F32)
        chunks = range(var * SPAN // 8, (var + 1) * SPAN // 8)
        for msg, skip, amount, start in parts:
            for piece in range(SEND):

                @pl.when(piece < amount)
                def _(msg=msg, piece=piece, start=start, skip=skip, chunks=chunks):
                    move(full, row_of(start + piece), TILE, msg, (skip + piece) * ROWS, 1, chunks)

        stores += block_copies(out, full, out_sems, range(TILES), var, False)
        for copy in stores[-TILES:]:
            copy.start()
    for copy in stores:
        copy.wait()


def final_kernel(mine, other, out):
    core = lax.axis_index("bal") % PAR_DEV
    out[pl.ds(core, FINE, stride=PAR_DEV), :] = mine[...]
    out[pl.ds(1 - core, FINE, stride=PAR_DEV), :] = other[...]


def call(kernel, outs, in_specs, args, out_specs, scratch=()):
    args = [
        pltpu.with_memory_space_constraint(arg, spec.memory_space) if spec in (VMEM, HBM) else arg
        for arg, spec in zip(args, in_specs, strict=True)
    ]
    kernel = pl.pallas_call(
        kernel,
        out_shape=outs,
        in_specs=in_specs,
        out_specs=out_specs,
        scratch_shapes=list(scratch),
        compiler_params=pltpu.CompilerParams(vmem_limit_bytes=12 << 20),
    )
    return kernel(*args)


def per_device(patches, patch_ids, live, counts, parent_of):
    slots = patches.shape[0]
    x = patches.transpose(1, 0, 2).reshape(VARS, TILES, TILE, SPAN, LANES)
    x = x.transpose(0, 1, 3, 2, 4).reshape(VARS, TILES, SPAN * TILE, LANES)
    counts = counts.reshape(-1)
    message = pltpu.VMEM((MSG, LANES), F32)
    dma = pltpu.SemaphoreType.DMA
    held, first, weight, info = call(
        load_kernel,
        (
            pltpu.VMEM((LIVE_TILES * TILE_ROWS, LANES), F32),
            message,
            pltpu.VMEM((4 * LANES, LANES), jnp.bfloat16),
            pltpu.VMEM((8, LANES), I32),
        ),
        [SMEM] + [HBM] * 4,
        (live, counts, patch_ids, parent_of, x),
        (VMEM,) * 4,
        [pltpu.SMEM(a.shape, I32) for a in (counts, patch_ids, parent_of)]
        + [dma((LIVE_TILES * VARS,)), dma((3,))],
    )
    came = from_partner(first, "bal", 1)
    half = pltpu.VMEM((NEAR_LEVELS * PIECE, LANES), F32)
    mine, other = call(
        restrict_kernel,
        (half, half),
        [VMEM] * 3,
        (info, held, weight),
        (VMEM, VMEM),
        [pltpu.VMEM((LIVE_TILES * TILE * FINE, LANES), F32)],
    )
    last, below = call(pick_kernel, (message, message), [VMEM] * 3, (info, held, came), (VMEM, VMEM))
    piece = pltpu.VMEM((PIECE, LANES), F32)
    pieces = call(
        add_kernel, (piece,) * NEAR_LEVELS, [VMEM, VMEM], (mine, from_partner(other, "bal", 1)), (VMEM,) * NEAR_LEVELS
    )
    partial = pieces[0]
    for mask in range(1, NEAR_LEVELS):
        partial = partial + from_partner(pieces[mask], "level", mask)
    far = from_partner(below, "bal", 4)
    near = from_partner(last, "bal", 2)
    cross = from_partner(last, "bal", 6)

    groups = [[z * NEAR_LEVELS + y for z in range(FAR_LEVELS)] for y in range(NEAR_LEVELS)]
    tiles = lax.all_to_all(
        partial.reshape(FAR_LEVELS, FINE // 4, 4, LANES), "level", 0, 0, axis_index_groups=groups, tiled=True
    )
    sums = jnp.sum(tiles, axis=0)
    sums = sums + from_partner(sums, "bal", 2) + from_partner(sums, "bal", 6) + from_partner(sums, "bal", 4)
    sums = sums.reshape(FINE, LANES)
    coarse = call(
        final_kernel,
        jax.ShapeDtypeStruct((FINE * PAR_DEV, LANES), F32),
        [VMEM, VMEM],
        (sums, from_partner(sums, "bal", 1)),
        VMEM,
    )
    coarse = coarse.reshape(VARS, FINE // VARS, PAR_DEV, LANES).transpose(2, 0, 1, 3).reshape(PAR_DEV, VARS, -1)

    out, new_ids = call(
        place_kernel,
        (jax.ShapeDtypeStruct((VARS, TILES, SPAN * TILE, LANES), F32), jax.ShapeDtypeStruct((1, slots), I32)),
        [VMEM, HBM, VMEM, VMEM, VMEM, VMEM],
        (info, x, came, near, far, cross),
        (HBM, VMEM),
        [pltpu.VMEM((TILES * TILE_ROWS, LANES), F32), dma((LIVE_TILES * VARS,)), dma((TILES * VARS,))],
    )
    out = out.reshape(VARS, TILES, SPAN, TILE, LANES).transpose(0, 1, 3, 2, 4)
    out = out.reshape(VARS, slots, SPAN * LANES).transpose(1, 0, 2)
    return (out, new_ids.reshape(slots), coarse)


def solution(mesh):
    return jax.shard_map(
        per_device,
        mesh=mesh,
        in_specs=(
            P(("level", "bal"), None, None),
            P(("level", "bal")),
            P(("level", "bal")),
            P(None, ("level", "bal")),
            P(),
        ),
        out_specs=(P(("level", "bal"), None, None), P(("level", "bal")), P("level", None, None)),
        check_vma=False,
    )
```

time: 58.6 us -> 54.7 us (0.933)
  Pallas kernels: 13.7 us -> 7.65 us
  starting transfers between devices: 22.7 us -> 28.7 us
  local copies, waits for them, and re-layouts: 3.97 us -> 0.01 us
  waiting for transfers between devices: 14.7 us -> 16.1 us
  other arithmetic: 1.58 us -> 0.69 us
    ppermute x8 -> x12, starting transfers between devices: 10.7 us -> 20.5 us  [from_partner(): lax.ppermute(array, axis, [(i, i ^ mask) for i in range(lax.axis_size(axi...]
    ppermute x8 -> x12, waiting for transfers between devices: 5.56 us -> 12.9 us  [from_partner(): lax.ppermute(array, axis, [(i, i ^ mask) for i in range(lax.axis_size(axi...]
    pallas_call x4 -> x6, Pallas kernels: 13.7 us -> 7.65 us  [call(): return kernel(*args)]
    all_to_all x1, waiting for transfers between devices: 9.14 us -> 3.2 us  [per_device(): lax.all_to_all(partial.reshape(FAR_LEVELS, FINE // 4, 4, LANES), 'level',...]
    all_to_all x1, starting transfers between devices: 12 us -> 8.24 us  [per_device(): lax.all_to_all(partial.reshape(FAR_LEVELS, FINE // 4, 4, LANES), 'level',...]
    unnamed x13 -> x0, local copies, waits for them, and re-layouts: 2.17 us -> none
    squeeze x1 -> x0, local copies, waits for them, and re-layouts: 1.18 us -> none  [per_device(): return (out, new_ids[0, :slots], coarse)]
    concatenate x1 -> x0, other arithmetic: 0.67 us -> none  [restriction_weight(): jnp.concatenate([jnp.where(target == group * 32 + column, 0.125, 0.0) for...]
  transfers between devices with their start and end apart: 9 -> 13, of which waited for: 4 -> 8; matrix products, arithmetic and copies ran while one was open for 3% -> 1% of each run, Pallas kernels for 12% -> 2%
where the time goes in v2:
time: 54.7 us; the launch traced here: 54.5 us
  starting transfers between devices  28.7 us (52%)
  waiting for transfers between devices  16.1 us (29%)
  Pallas kernels  7.65 us (14%)
  between operations  1.34 us (2%)
  other arithmetic  0.69 us (1%)
    ppermute x12, starting transfers between devices, from_partner(): lax.ppermute(array, axis, [(i, i ^ mask) for i in range(lax.axis_size(axi...  20.5 us
    ppermute x12, waiting for transfers between devices, from_partner(): lax.ppermute(array, axis, [(i, i ^ mask) for i in range(lax.axis_size(axi...  12.9 us
    all_to_all x1, starting transfers between devices, per_device(): lax.all_to_all(partial.reshape(FAR_LEVELS, FINE // 4, 4, LANES), 'level',...  8.24 us
    pallas_call x6, Pallas kernels, call(): return kernel(*args)  7.65 us
    all_to_all x1, waiting for transfers between devices, per_device(): lax.all_to_all(partial.reshape(FAR_LEVELS, FINE // 4, 4, LANES), 'level',...  3.2 us
  transfers between devices with their start and end apart: 13, of which 8 were waited for; matrix products, arithmetic and copies ran while one was open for 1% of the time, Pallas kernels for 2%

profile of v2, /device:TPU:1, one launch (start us, length us, event | category | flops | bytes accessed | tf_op | source)
XLA Modules:
  0.0 54.5 jit_solution(12164873629502680216)
XLA Ops:
  1.3 1.6 %shard_map.76 = (f32[2560,128]{1,0:T(8,128)S(1)}, f32[648,128]{1,0:T(8,128)S(1)}, bf16[512,128]{1,0:T(8,128)(2,1)S(1)}, s32[8,128]{1,0:T(8,128)S(1)}) custom-call(s32[1]{0:T(128)S(6)} %copy.9.live, s32[3]{0:T(128)} %bitcast.25, s32[24]{0:T(128)} %ids.1, s32[6144]{0:T(1024)} %parent_of.1, f32[5,3,256,128]{3,2,1,0:T(8,128)} %bitcast.22), custom_call_target="tpu_custom_call" | custom-call | tf_op jit(solution)/shard_map/pallas_call | solution.py:274
  2.9 1.7 %shard_map.79 = (f32[640,128]{1,0:T(8,128)S(1)}, f32[640,128]{1,0:T(8,128)S(1)}) custom-call(s32[8,128]{1,0:T(8,128)S(1)} %get-tuple-element.17.info, f32[2560,128]{1,0:T(8,128)S(1)} %get-tuple-element.19.held, bf16[512,128]{1,0:T(8,128)(2,1)S(1)} %get-tuple-element.24.weight), custom_call_target="tpu_custom_call" | custom-call | tf_op jit(solution)/shard_map/pallas_call | solution.py:274
  4.6 3.3 %collective-permute-start.4 = (f32[640,128]{1,0:T(8,128)S(1)}, f32[640,128]{1,0:T(8,128)S(1)}, u32[]{:S(2)}, u32[]{:S(2)}) collective-permute-start(f32[640,128]{1,0:T(8,128)S(1)} %get-tuple-element.26), channel_id=1, source_target_pairs={{0,1},{1,0},{2,3},{3,2},{4,5},{5,4},{6,7},{7,6},{8,9},{9,8},{10,11... | collective-permute-start | bytes 983048 | tf_op jit(solution)/shard_map/ppermute | solution.py:38
  7.8 1.3 %collective-permute-done.4.other = f32[640,128]{1,0:T(8,128)S(1)} collective-permute-done((f32[640,128]{1,0:T(8,128)S(1)}, f32[640,128]{1,0:T(8,128)S(1)}, u32[]{:S(2)}, u32[]{:S(2)}) %collective-permute-start.4) | collective-permute-done | bytes 327712 | tf_op jit(solution)/shard_map/ppermute | solution.py:38
  9.1 0.1 collective-permute-start.5
  9.2 2.2 %collective-permute-start.6 = (f32[160,128]{1,0:T(8,128)S(1)}, f32[160,128]{1,0:T(8,128)S(1)}, u32[]{:S(2)}, u32[]{:S(2)}) collective-permute-start(f32[160,128]{1,0:T(8,128)S(1)} %get-tuple-element.29), channel_id=1, source_target_pairs={{0,16},{8,24},{16,0},{24,8},{32,48},{40,56},{48,32},{56,40},{64,80... | collective-permute-start | bytes 245768 | tf_op jit(solution)/shard_map/ppermute | solution.py:38
  11.4 1.7 %collective-permute-start.7 = (f32[160,128]{1,0:T(8,128)S(1)}, f32[160,128]{1,0:T(8,128)S(1)}, u32[]{:S(2)}, u32[]{:S(2)}) collective-permute-start(f32[160,128]{1,0:T(8,128)S(1)} %get-tuple-element.30), channel_id=1, source_target_pairs={{0,24},{8,16},{16,8},{24,0},{32,56},{40,48},{48,40},{56,32},{64,88... | collective-permute-start | bytes 245768 | tf_op jit(solution)/shard_map/ppermute | solution.py:38
  13.1 1.2 %collective-permute-start = (f32[648,128]{1,0:T(8,128)S(1)}, f32[648,128]{1,0:T(8,128)S(1)}, u32[]{:S(2)}, u32[]{:S(2)}) collective-permute-start(f32[648,128]{1,0:T(8,128)S(1)} %get-tuple-element.18), channel_id=1, source_target_pairs={{0,1},{1,0},{2,3},{3,2},{4,5},{5,4},{6,7},{7,6},{8,9},{9,8},{10,11... | collective-permute-start | bytes 995336 | tf_op jit(solution)/shard_map/ppermute | solution.py:38
  14.3 0.0 collective-permute-done.5
  14.3 1.0 %collective-permute-done.6 = f32[160,128]{1,0:T(8,128)S(1)} collective-permute-done((f32[160,128]{1,0:T(8,128)S(1)}, f32[160,128]{1,0:T(8,128)S(1)}, u32[]{:S(2)}, u32[]{:S(2)}) %collective-permute-start.6) | collective-permute-done | bytes 81952 | tf_op jit(solution)/shard_map/ppermute | solution.py:38
  15.3 2.0 %collective-permute-done.7 = f32[160,128]{1,0:T(8,128)S(1)} collective-permute-done((f32[160,128]{1,0:T(8,128)S(1)}, f32[160,128]{1,0:T(8,128)S(1)}, u32[]{:S(2)}, u32[]{:S(2)}) %collective-permute-start.7) | collective-permute-done | bytes 81952 | tf_op jit(solution)/shard_map/ppermute | solution.py:38
  17.4 0.7 %add_add_fusion = f32[160,128]{1,0:T(8,128)} fusion(f32[160,128]{1,0:T(8,128)S(1)} %collective-permute-done.7, f32[160,128]{1,0:T(8,128)S(1)} %collective-permute-done.6, f32[160,128]{1,0:T(8,128)S(1)} %get-tuple-element.27, f32[160,128]{1,0:T(8,128)S(1)} %collective-permute-done.5), kind=kLoop, calls=%fused_computation | loop fusion | flops 61440 | bytes 409600 | tf_op jit(solution)/shard_map/add | solution.py:315
  18.0 8.2 %all-to-all-start = ((f32[8,5,4,128]{3,2,1,0:T(4,128)}), f32[8,5,4,128]{3,2,1,0:T(4,128)S(1)}, u32[]{:S(2)}, u32[]{:S(2)}) async-start(f32[8,5,4,128]{3,2,1,0:T(4,128)} %bitcast.10), calls=%async_computation | async-start | bytes 163840 | tf_op jit(solution)/shard_map/all_to_all | solution.py:321
  26.3 0.0 collective-permute-done.came
  26.3 0.5 shard_map.77
  26.8 2.7 %collective-permute-start.2 = (f32[648,128]{1,0:T(8,128)S(1)}, f32[648,128]{1,0:T(8,128)S(1)}, u32[]{:S(2)}, u32[]{:S(2)}) collective-permute-start(f32[648,128]{1,0:T(8,128)S(1)} %get-tuple-element.21), channel_id=1, source_target_pairs={{0,4},{1,5},{2,6},{3,7},{4,0},{5,1},{6,2},{7,3},{8,12},{9,13},{10,... | collective-permute-start | bytes 995336 | tf_op jit(solution)/shard_map/ppermute | solution.py:38
  29.5 1.0 %collective-permute-start.3 = (f32[648,128]{1,0:T(8,128)S(1)}, f32[648,128]{1,0:T(8,128)S(1)}, u32[]{:S(2)}, u32[]{:S(2)}) collective-permute-start(f32[648,128]{1,0:T(8,128)S(1)} %get-tuple-element.20), channel_id=1, source_target_pairs={{0,6},{1,7},{2,4},{3,5},{4,2},{5,3},{6,0},{7,1},{8,14},{9,15},{10,... | collective-permute-start | bytes 995336 | tf_op jit(solution)/shard_map/ppermute | solution.py:38
  30.5 0.0 collective-permute-start.1
  30.5 3.2 %all-to-all-done = f32[8,5,4,128]{3,2,1,0:T(4,128)S(1)} async-done(((f32[8,5,4,128]{3,2,1,0:T(4,128)}), f32[8,5,4,128]{3,2,1,0:T(4,128)S(1)}, u32[]{:S(2)}, u32[]{:S(2)}) %all-to-all-start) | async-done | bytes 81952 | tf_op jit(solution)/shard_map/all_to_all | solution.py:321
  33.7 2.8 %collective-permute-start.10 = (f32[5,4,128]{2,1,0:T(4,128)S(1)}, f32[5,4,128]{2,1,0:T(4,128)S(1)}, u32[]{:S(2)}, u32[]{:S(2)}) collective-permute-start(f32[5,4,128]{2,1,0:T(4,128)S(1)} %reduce_sum.9), channel_id=1, source_target_pairs={{0,4},{1,5},{2,6},{3,7},{4,0},{5,1},{6,2},{7,3},{8,12},{9,13},{10,... | collective-permute-start | bytes 30728 | tf_op jit(solution)/shard_map/ppermute | solution.py:38
  36.5 0.9 %collective-permute-start.9 = (f32[5,4,128]{2,1,0:T(4,128)S(1)}, f32[5,4,128]{2,1,0:T(4,128)S(1)}, u32[]{:S(2)}, u32[]{:S(2)}) collective-permute-start(f32[5,4,128]{2,1,0:T(4,128)S(1)} %reduce_sum.9), channel_id=1, source_target_pairs={{0,6},{1,7},{2,4},{3,5},{4,2},{5,3},{6,0},{7,1},{8,14},{9,15},{10,... | collective-permute-start | bytes 30728 | tf_op jit(solution)/shard_map/ppermute | solution.py:38
  37.4 6.3 %collective-permute-done.10 = f32[5,4,128]{2,1,0:T(4,128)S(1)} collective-permute-done((f32[5,4,128]{2,1,0:T(4,128)S(1)}, f32[5,4,128]{2,1,0:T(4,128)S(1)}, u32[]{:S(2)}, u32[]{:S(2)}) %collective-permute-start.10) | collective-permute-done | bytes 10272 | tf_op jit(solution)/shard_map/ppermute | solution.py:38
  43.7 1.1 %collective-permute-start.8 = (f32[5,4,128]{2,1,0:T(4,128)S(1)}, f32[5,4,128]{2,1,0:T(4,128)S(1)}, u32[]{:S(2)}, u32[]{:S(2)}) collective-permute-start(f32[5,4,128]{2,1,0:T(4,128)S(1)} %reduce_sum.9), channel_id=1, source_target_pairs={{0,2},{1,3},{2,0},{3,1},{4,6},{5,7},{6,4},{7,5},{8,10},{9,11},{10,... | collective-permute-start | bytes 30728 | tf_op jit(solution)/shard_map/ppermute | solution.py:38
  44.8 0.8 %collective-permute-done.9 = f32[5,4,128]{2,1,0:T(4,128)S(1)} collective-permute-done((f32[5,4,128]{2,1,0:T(4,128)S(1)}, f32[5,4,128]{2,1,0:T(4,128)S(1)}, u32[]{:S(2)}, u32[]{:S(2)}) %collective-permute-start.9) | collective-permute-done | bytes 10272 | tf_op jit(solution)/shard_map/ppermute | solution.py:38
  45.6 0.6 %collective-permute-done.8 = f32[5,4,128]{2,1,0:T(4,128)S(1)} collective-permute-done((f32[5,4,128]{2,1,0:T(4,128)S(1)}, f32[5,4,128]{2,1,0:T(4,128)S(1)}, u32[]{:S(2)}, u32[]{:S(2)}) %collective-permute-start.8) | collective-permute-done | bytes 10272 | tf_op jit(solution)/shard_map/ppermute | solution.py:38
  46.2 3.6 %collective-permute-start.11 = (f32[20,128]{1,0:T(8,128)S(1)}, f32[20,128]{1,0:T(8,128)S(1)}, u32[]{:S(2)}, u32[]{:S(2)}) collective-permute-start(f32[20,128]{1,0:T(8,128)S(1)} %reshape.43.mine), channel_id=1, source_target_pairs={{0,1},{1,0},{2,3},{3,2},{4,5},{5,4},{6,7},{7,6},{8,9},{9,8},{10,11... | collective-permute-start | bytes 30728 | tf_op jit(solution)/shard_map/ppermute | solution.py:38
  49.9 0.8 %collective-permute-done.11.other = f32[20,128]{1,0:T(8,128)S(1)} collective-permute-done((f32[20,128]{1,0:T(8,128)S(1)}, f32[20,128]{1,0:T(8,128)S(1)}, u32[]{:S(2)}, u32[]{:S(2)}) %collective-permute-start.11) | collective-permute-done | bytes 10272 | tf_op jit(solution)/shard_map/ppermute | solution.py:38
  50.7 0.6 %shard_map.81 = f32[40,128]{1,0:T(8,128)} custom-call(f32[20,128]{1,0:T(8,128)S(1)} %reshape.43.mine, f32[20,128]{1,0:T(8,128)S(1)} %collective-permute-done.11.other), custom_call_target="tpu_custom_call" | custom-call | tf_op jit(solution)/shard_map/pallas_call | solution.py:274
  51.3 0.0 collective-permute-done.2.far
  51.3 0.0 collective-permute-done.3.cross
  51.3 0.0 collective-permute-done.1.near
  51.3 3.2 %shard_map.78 = (f32[5,3,256,128]{3,2,1,0:T(8,128)}, s32[1,24]{1,0:T(1,128)}) custom-call(s32[8,128]{1,0:T(8,128)S(1)} %get-tuple-element.17.info, f32[5,3,256,128]{3,2,1,0:T(8,128)} %bitcast.23, f32[648,128]{1,0:T(8,128)S(1)} %collective-permute-done.came, f32[648,128]{1,0:T(8,128)S(1)} %collective-permute-done.1.near, ...), custom_call_target="tpu_custom_call" | custom-call | tf_op jit(solution)/shard_map/pallas_call | solution.py:274
  (4 shorter events, 0.1 us)
Async XLA Ops:
  4.6 4.5 %collective-permute-start.4 = (f32[640,128]{1,0:T(8,128)S(1)}, f32[640,128]{1,0:T(8,128)S(1)}, u32[]{:S(2)}, u32[]{:S(2)}) collective-permute-start(f32[640,128]{1,0:T(8,128)S(1)} %get-tuple-element.26), channel_id=1, source_target_pairs={{0,1},{1,0},{2,3},{3,2},{4,5},{5,4},{6,7},{7,6},{8,9},{9,8},{10,11... | collective-permute-start | bytes 983048 | tf_op jit(solution)/shard_map/ppermute | solution.py:38
  9.1 5.2 %collective-permute-start.5 = (f32[160,128]{1,0:T(8,128)S(1)}, f32[160,128]{1,0:T(8,128)S(1)}, u32[]{:S(2)}, u32[]{:S(2)}) collective-permute-start(f32[160,128]{1,0:T(8,128)S(1)} %get-tuple-element.28), channel_id=1, source_target_pairs={{0,8},{8,0},{16,24},{24,16},{32,40},{40,32},{48,56},{56,48},{64,72... | collective-permute-start | bytes 245768 | tf_op jit(solution)/shard_map/ppermute | solution.py:38
  9.2 6.1 %collective-permute-start.6 = (f32[160,128]{1,0:T(8,128)S(1)}, f32[160,128]{1,0:T(8,128)S(1)}, u32[]{:S(2)}, u32[]{:S(2)}) collective-permute-start(f32[160,128]{1,0:T(8,128)S(1)} %get-tuple-element.29), channel_id=1, source_target_pairs={{0,16},{8,24},{16,0},{24,8},{32,48},{40,56},{48,32},{56,40},{64,80... | collective-permute-start | bytes 245768 | tf_op jit(solution)/shard_map/ppermute | solution.py:38
  11.4 5.9 %collective-permute-start.7 = (f32[160,128]{1,0:T(8,128)S(1)}, f32[160,128]{1,0:T(8,128)S(1)}, u32[]{:S(2)}, u32[]{:S(2)}) collective-permute-start(f32[160,128]{1,0:T(8,128)S(1)} %get-tuple-element.30), channel_id=1, source_target_pairs={{0,24},{8,16},{16,8},{24,0},{32,56},{40,48},{48,40},{56,32},{64,88... | collective-permute-start | bytes 245768 | tf_op jit(solution)/shard_map/ppermute | solution.py:38
  13.1 13.2 %collective-permute-start = (f32[648,128]{1,0:T(8,128)S(1)}, f32[648,128]{1,0:T(8,128)S(1)}, u32[]{:S(2)}, u32[]{:S(2)}) collective-permute-start(f32[648,128]{1,0:T(8,128)S(1)} %get-tuple-element.18), channel_id=1, source_target_pairs={{0,1},{1,0},{2,3},{3,2},{4,5},{5,4},{6,7},{7,6},{8,9},{9,8},{10,11... | collective-permute-start | bytes 995336 | tf_op jit(solution)/shard_map/ppermute | solution.py:38
  18.0 15.7 %all-to-all-start = ((f32[8,5,4,128]{3,2,1,0:T(4,128)}), f32[8,5,4,128]{3,2,1,0:T(4,128)S(1)}, u32[]{:S(2)}, u32[]{:S(2)}) async-start(f32[8,5,4,128]{3,2,1,0:T(4,128)} %bitcast.10), calls=%async_computation | async-start | bytes 163840 | tf_op jit(solution)/shard_map/all_to_all | solution.py:321
  26.8 24.5 %collective-permute-start.2 = (f32[648,128]{1,0:T(8,128)S(1)}, f32[648,128]{1,0:T(8,128)S(1)}, u32[]{:S(2)}, u32[]{:S(2)}) collective-permute-start(f32[648,128]{1,0:T(8,128)S(1)} %get-tuple-element.21), channel_id=1, source_target_pairs={{0,4},{1,5},{2,6},{3,7},{4,0},{5,1},{6,2},{7,3},{8,12},{9,13},{10,... | collective-permute-start | bytes 995336 | tf_op jit(solution)/shard_map/ppermute | solution.py:38
  29.5 21.8 %collective-permute-start.3 = (f32[648,128]{1,0:T(8,128)S(1)}, f32[648,128]{1,0:T(8,128)S(1)}, u32[]{:S(2)}, u32[]{:S(2)}) collective-permute-start(f32[648,128]{1,0:T(8,128)S(1)} %get-tuple-element.20), channel_id=1, source_target_pairs={{0,6},{1,7},{2,4},{3,5},{4,2},{5,3},{6,0},{7,1},{8,14},{9,15},{10,... | collective-permute-start | bytes 995336 | tf_op jit(solution)/shard_map/ppermute | solution.py:38
  30.5 20.9 %collective-permute-start.1 = (f32[648,128]{1,0:T(8,128)S(1)}, f32[648,128]{1,0:T(8,128)S(1)}, u32[]{:S(2)}, u32[]{:S(2)}) collective-permute-start(f32[648,128]{1,0:T(8,128)S(1)} %get-tuple-element.20), channel_id=1, source_target_pairs={{0,2},{1,3},{2,0},{3,1},{4,6},{5,7},{6,4},{7,5},{8,10},{9,11},{10,... | collective-permute-start | bytes 995336 | tf_op jit(solution)/shard_map/ppermute | solution.py:38
  33.7 10.0 %collective-permute-start.10 = (f32[5,4,128]{2,1,0:T(4,128)S(1)}, f32[5,4,128]{2,1,0:T(4,128)S(1)}, u32[]{:S(2)}, u32[]{:S(2)}) collective-permute-start(f32[5,4,128]{2,1,0:T(4,128)S(1)} %reduce_sum.9), channel_id=1, source_target_pairs={{0,4},{1,5},{2,6},{3,7},{4,0},{5,1},{6,2},{7,3},{8,12},{9,13},{10,... | collective-permute-start | bytes 30728 | tf_op jit(solution)/shard_map/ppermute | solution.py:38
  36.5 9.1 %collective-permute-start.9 = (f32[5,4,128]{2,1,0:T(4,128)S(1)}, f32[5,4,128]{2,1,0:T(4,128)S(1)}, u32[]{:S(2)}, u32[]{:S(2)}) collective-permute-start(f32[5,4,128]{2,1,0:T(4,128)S(1)} %reduce_sum.9), channel_id=1, source_target_pairs={{0,6},{1,7},{2,4},{3,5},{4,2},{5,3},{6,0},{7,1},{8,14},{9,15},{10,... | collective-permute-start | bytes 30728 | tf_op jit(solution)/shard_map/ppermute | solution.py:38
  43.7 2.5 %collective-permute-start.8 = (f32[5,4,128]{2,1,0:T(4,128)S(1)}, f32[5,4,128]{2,1,0:T(4,128)S(1)}, u32[]{:S(2)}, u32[]{:S(2)}) collective-permute-start(f32[5,4,128]{2,1,0:T(4,128)S(1)} %reduce_sum.9), channel_id=1, source_target_pairs={{0,2},{1,3},{2,0},{3,1},{4,6},{5,7},{6,4},{7,5},{8,10},{9,11},{10,... | collective-permute-start | bytes 30728 | tf_op jit(solution)/shard_map/ppermute | solution.py:38
  46.2 4.5 %collective-permute-start.11 = (f32[20,128]{1,0:T(8,128)S(1)}, f32[20,128]{1,0:T(8,128)S(1)}, u32[]{:S(2)}, u32[]{:S(2)}) collective-permute-start(f32[20,128]{1,0:T(8,128)S(1)} %reshape.43.mine), channel_id=1, source_target_pairs={{0,1},{1,0},{2,3},{3,2},{4,5},{5,4},{6,7},{7,6},{8,9},{9,8},{10,11... | collective-permute-start | bytes 30728 | tf_op jit(solution)/shard_map/ppermute | solution.py:38

commit v3 on v2

v3 whole, which is shorter than its diff:
```python
import jax
import jax.numpy as jnp
from jax import lax
from jax.experimental import pallas as pl
from jax.experimental.pallas import tpu as pltpu
from jax.sharding import PartitionSpec as P


VARS = 5
SEND = 4
TILE = 8
TILES = 3
LIVE_TILES = 2
LIVE = 12
LANES = 128
SPAN = 32
ROWS = VARS * SPAN
TILE_ROWS = ROWS * TILE
HEAD = SEND * ROWS
MSG = HEAD + 8
FINE = 20
PAR_DEV = 2
F32 = jnp.float32
I32 = jnp.int32
LIVE_AT = 16
COUNTS_AT = 17

SMEM = pl.BlockSpec(memory_space=pltpu.SMEM)
VMEM = pl.BlockSpec(memory_space=pltpu.VMEM)
HBM = pl.BlockSpec(memory_space=pltpu.HBM)


def from_partner(array, axis, mask):
    return lax.ppermute(array, axis, [(i, i ^ mask) for i in range(lax.axis_size(axis))])


def lanes():
    return lax.broadcasted_iota(I32, (8, LANES), 1)


def row_of(slot):
    return (slot // TILE) * TILE_ROWS + slot % TILE


def fill_weight(weight):
    lane = lax.broadcasted_iota(I32, (LANES, LANES), 0)
    target = lax.broadcasted_iota(I32, (LANES, LANES), 1)
    column = (lane // 32) * 8 + (lane % 16) // 2
    for group in range(4):
        part = jnp.where(target == group * 32 + column, 0.125, 0.0)
        weight[pl.ds(group * LANES, LANES), :] = part.astype(jnp.bfloat16)


def rows_at(row, step, chunk):
    start = row + chunk * 8 * step
    if step == 1:
        return pl.ds(pl.multiple_of(start, 8), 8)
    return pl.ds(start, 8, stride=step)


def move(dst, dst_row, dst_step, src, src_row, src_step, chunks=range(ROWS // 8)):
    for chunk in chunks:
        dst[rows_at(dst_row, dst_step, chunk), :] = src[rows_at(src_row, src_step, chunk), :]


def block_copies(hbm, vmem, sems, tiles, var, inward):
    copies = []
    for tile in tiles:
        part = vmem.at[pl.ds((tile * VARS + var) * SPAN * TILE, SPAN * TILE), :]
        ends = (hbm.at[var, tile], part) if inward else (part, hbm.at[var, tile])
        copies.append(pltpu.make_async_copy(*ends, sems.at[tile * VARS + var]))
    return copies


def load_kernel(
    live, counts, ids, parent_of, x, held, msg, info, mine, other,
    counts_s, ids_s, parents, weight, fine, both, sems, small_sems,
):
    small = [
        pltpu.make_async_copy(src, dst, small_sems.at[i])
        for i, (src, dst) in enumerate(((counts, counts_s), (ids, ids_s), (parent_of, parents)))
    ]
    for copy in small:
        copy.start()
    copies = []
    for var in range(VARS):
        copies += block_copies(x, held, sems, range(LIVE_TILES), var, True)
    for copy in copies:
        copy.start()
    fill_weight(weight)
    both[...] = jnp.zeros_like(both)
    for copy in small:
        copy.wait()
    sent = counts_s[0]
    first = live[0] - sent
    lane = lanes()
    head = jnp.where(lane == SEND, sent.astype(F32), 0.0)
    for lane_id in range(SEND):
        slot = jnp.minimum(first + lane_id, LIVE - 1)
        head = jnp.where(lane == lane_id, ids_s[slot].astype(F32), head)
    msg[pl.ds(HEAD, 8), :] = head
    numbers = jnp.where(lane == LIVE_AT, live[0], 0)
    for turn in range(3):
        numbers = jnp.where(lane == COUNTS_AT + turn, counts_s[turn], numbers)
    half = mine.shape[0]
    core = lax.axis_index("bal") % PAR_DEV
    bases = []
    for slot in range(LIVE):
        mark = ids_s[slot]
        numbers = jnp.where(lane == slot, mark, numbers)
        parent = parents[mark]
        base = (parent // PAR_DEV) * FINE + jnp.bitwise_xor(parent % PAR_DEV, core) * half
        bases.append(jnp.where(slot < live[0], base, PAR_DEV * half))
    info[...] = numbers
    for copy in copies:
        copy.wait()

    groups = LIVE_TILES * VARS * SPAN // 8
    rows = held[...].reshape(groups, 8, TILE, LANES)
    pieces = []
    for side in range(4):
        at = side // 2 * 4 + side % 2
        pieces.append((rows[:, at] + rows[:, at + 2]).reshape(groups * TILE, LANES))
    pairs = jnp.concatenate(pieces, axis=1)
    high = pairs.astype(jnp.bfloat16)
    low = (pairs - high.astype(F32)).astype(jnp.bfloat16)
    w = weight[...]
    fine[...] = jnp.dot(high, w, preferred_element_type=F32) + jnp.dot(low, w, preferred_element_type=F32)
    for slot, base in enumerate(bases):
        src = (slot // TILE) * (FINE * TILE) + slot % TILE
        for start, size in ((0, 8), (8, 8), (16, 4)):
            both[pl.ds(base + start, size), :] += fine[pl.ds(src + start * TILE, size, stride=TILE), :]
    mine[...] = both[pl.ds(0, half), :]
    other[...] = both[pl.ds(half, half), :]
    for piece in range(SEND):

        @pl.when(piece < sent)
        def _(piece=piece):
            move(msg, piece * ROWS, 1, held, row_of(first + piece), TILE)


def add_kernel(mine, other, out):
    out[...] = mine[...] + other[...]


def number(ref, lane):
    return ref[HEAD, lane].astype(I32)


def head_of(ref):
    return ref[pl.ds(HEAD, 8), :]


def pick_kernel(info, held, came, last, below):
    lane = lanes()
    sent = info[0, COUNTS_AT + 1]
    kept = info[0, LIVE_AT] - info[0, COUNTS_AT]
    held_count = kept + number(came, SEND)
    marks = info[...].astype(F32)
    marks = jnp.where(lane < kept, marks, pltpu.roll(head_of(came), kept, 1))
    for msg, first, pieces in ((last, held_count - sent, sent), (below, held_count - sent - SEND, SEND)):
        head = pltpu.roll(marks, lax.rem(LANES - first, LANES), 1)
        head = jnp.where(lane == SEND, sent.astype(F32), head)
        head = jnp.where(lane == SEND + 1, info[0, COUNTS_AT + 2].astype(F32), head)
        msg[pl.ds(HEAD, 8), :] = head
        for piece in range(SEND):
            slot = first + piece
            used = jnp.logical_and(slot >= 0, piece < pieces)

            @pl.when(jnp.logical_and(used, slot < kept))
            def _(msg=msg, piece=piece, slot=slot):
                move(msg, piece * ROWS, 1, held, row_of(slot), TILE)

            @pl.when(jnp.logical_and(used, slot >= kept))
            def _(msg=msg, piece=piece, slot=slot):
                move(msg, piece * ROWS, 1, came, (slot - kept) * ROWS, 1)


def base_kernel(info, x, out, full, in_sems, out_sems):
    loads = [block_copies(x, full, in_sems, range(LIVE_TILES), var, True) for var in range(VARS)]
    for copies in loads:
        for copy in copies:
            copy.start()
    kept = info[0, LIVE_AT] - info[0, COUNTS_AT]
    sub = lax.broadcasted_iota(I32, (TILE, LANES), 0)
    full[pl.ds(LIVE_TILES * TILE_ROWS, TILE_ROWS), :] = jnp.zeros((TILE_ROWS, LANES), F32)
    stores = []
    for var in range(VARS):
        for copy in loads[var]:
            copy.wait()
        for tile in range(LIVE_TILES):
            rows = pl.ds((tile * VARS + var) * SPAN * TILE, SPAN * TILE)
            part = full[rows, :].reshape(SPAN, TILE, LANES)
            keep = (sub + tile * TILE < kept)[None]
            full[rows, :] = jnp.where(keep, part, 0.0).reshape(SPAN * TILE, LANES)
        stores += block_copies(out, full, out_sems, range(TILES), var, False)
        for copy in stores[-TILES:]:
            copy.start()
    for copy in stores:
        copy.wait()


def place_kernel(info, came, near, far, cross, base, out, new_ids, blank, sems):
    del base
    blank[...] = jnp.zeros_like(blank)
    lane = lanes()
    kept = info[0, LIVE_AT] - info[0, COUNTS_AT]
    c0 = number(came, SEND)
    c1, c2 = info[0, COUNTS_AT + 1], info[0, COUNTS_AT + 2]
    n1 = number(near, SEND)
    f2 = number(far, SEND + 1)
    x1 = number(cross, SEND)
    own = kept + c0 - c1 - jnp.maximum(c2 - n1, 0)
    from_near = jnp.maximum(n1 - c2, 0)
    from_far = jnp.maximum(f2 - x1, 0)
    from_cross = jnp.minimum(x1, f2)
    bare = jnp.minimum(own, kept)

    def copy_of(msg, row, slot, sem):
        return pltpu.make_async_copy(
            msg.at[pl.ds(row, ROWS), :].reshape(VARS, SPAN, LANES), out.at[:, slot // TILE, :, slot % TILE], sem
        )

    copies = []
    start = bare
    new = jnp.where(lane < bare, info[...].astype(F32), -1.0)
    for msg, skip, amount in (
        (came, 0, own - bare),
        (near, 0, from_near),
        (far, SEND - from_far, from_far),
        (cross, x1 - from_cross, from_cross),
    ):
        for piece in range(SEND):
            row = pl.multiple_of((skip + piece) * ROWS, 8)
            copies.append((piece < amount, msg, row, start + piece))
        moved = pltpu.roll(head_of(msg), lax.rem(start - skip + LANES, LANES), 1)
        new = jnp.where(jnp.logical_and(lane >= start, lane < start + amount), moved, new)
        start = start + amount
    copies += [(start + piece < kept, blank, 0, start + piece) for piece in range(2 * SEND)]
    for i, (used, *ends) in enumerate(copies):

        @pl.when(used)
        def _(i=i, ends=ends):
            copy_of(*ends, sems.at[i]).start()

    new_ids[...] = new[0:1, : TILE * TILES].astype(I32)
    for i, (used, *ends) in enumerate(copies):

        @pl.when(used)
        def _(i=i, ends=ends):
            copy_of(*ends, sems.at[i]).wait()


def final_kernel(mine, other, out):
    core = lax.axis_index("bal") % PAR_DEV
    out[pl.ds(core, FINE, stride=PAR_DEV), :] = mine[...]
    out[pl.ds(1 - core, FINE, stride=PAR_DEV), :] = other[...]


def call(kernel, outs, in_specs, args, out_specs, scratch=(), aliases={}):
    args = [
        pltpu.with_memory_space_constraint(arg, spec.memory_space) if spec in (VMEM, HBM) else arg
        for arg, spec in zip(args, in_specs, strict=True)
    ]
    kernel = pl.pallas_call(
        kernel,
        out_shape=outs,
        in_specs=in_specs,
        out_specs=out_specs,
        scratch_shapes=list(scratch),
        compiler_params=pltpu.CompilerParams(vmem_limit_bytes=12 << 20),
        input_output_aliases=aliases,
    )
    return kernel(*args)


def per_device(patches, patch_ids, live, counts, parent_of):
    slots = patches.shape[0]
    x = patches.transpose(1, 0, 2).reshape(VARS, TILES, TILE, SPAN, LANES)
    x = x.transpose(0, 1, 3, 2, 4).reshape(VARS, TILES, SPAN * TILE, LANES)
    counts = counts.reshape(-1)
    message = pltpu.VMEM((MSG, LANES), F32)
    dma = pltpu.SemaphoreType.DMA
    levels = lax.axis_size("level")
    half = pltpu.VMEM((levels * FINE, LANES), F32)
    held, first, info, mine, other = call(
        load_kernel,
        (pltpu.VMEM((LIVE_TILES * TILE_ROWS, LANES), F32), message, pltpu.VMEM((8, LANES), I32), half, half),
        [SMEM] + [HBM] * 4,
        (live, counts, patch_ids, parent_of, x),
        (VMEM,) * 5,
        [pltpu.SMEM(a.shape, I32) for a in (counts, patch_ids, parent_of)]
        + [
            pltpu.VMEM((4 * LANES, LANES), jnp.bfloat16),
            pltpu.VMEM((LIVE_TILES * TILE * FINE, LANES), F32),
            pltpu.VMEM((PAR_DEV * levels * FINE + 24, LANES), F32),
            dma((LIVE_TILES * VARS,)),
            dma((3,)),
        ],
    )
    came = from_partner(first, "bal", 1)
    last, below = call(pick_kernel, (message, message), [VMEM] * 3, (info, held, came), (VMEM, VMEM))
    partial = call(add_kernel, half, [VMEM, VMEM], (mine, from_partner(other, "bal", 1)), VMEM)
    far = from_partner(below, "bal", 4)
    near = from_partner(last, "bal", 2)
    cross = from_partner(last, "bal", 6)

    tiles = lax.all_to_all(partial.reshape(levels, FINE // 4, 4, LANES), "level", 0, 0, tiled=True)
    sums = jnp.sum(tiles, axis=0)
    sums = sums + from_partner(sums, "bal", 2) + from_partner(sums, "bal", 6) + from_partner(sums, "bal", 4)
    sums = sums.reshape(FINE, LANES)
    coarse = call(
        final_kernel,
        jax.ShapeDtypeStruct((FINE * PAR_DEV, LANES), F32),
        [VMEM, VMEM],
        (sums, from_partner(sums, "bal", 1)),
        VMEM,
    )
    coarse = coarse.reshape(VARS, FINE // VARS, PAR_DEV, LANES).transpose(2, 0, 1, 3).reshape(PAR_DEV, VARS, -1)

    base = call(
        base_kernel,
        jax.ShapeDtypeStruct((VARS, TILES, SPAN * TILE, LANES), F32),
        [VMEM, HBM],
        (info, x),
        HBM,
        [pltpu.VMEM((TILES * TILE_ROWS, LANES), F32), dma((LIVE_TILES * VARS,)), dma((TILES * VARS,))],
    )
    spread_out = (VARS, TILES, SPAN, TILE, LANES)
    out, new_ids = call(
        place_kernel,
        (jax.ShapeDtypeStruct(spread_out, F32), jax.ShapeDtypeStruct((1, slots), I32)),
        [VMEM, VMEM, VMEM, VMEM, VMEM, HBM],
        (info, came, near, far, cross, base.reshape(spread_out)),
        (HBM, VMEM),
        [pltpu.VMEM((ROWS, LANES), F32), dma((6 * SEND,))],
        {5: 0},
    )
    out = out.transpose(0, 1, 3, 2, 4)
    out = out.reshape(VARS, slots, SPAN * LANES).transpose(1, 0, 2)
    return (out, new_ids.reshape(slots), coarse)


def solution(mesh):
    return jax.shard_map(
        per_device,
        mesh=mesh,
        in_specs=(
            P(("level", "bal"), None, None),
            P(("level", "bal")),
            P(("level", "bal")),
            P(None, ("level", "bal")),
            P(),
        ),
        out_specs=(P(("level", "bal"), None, None), P(("level", "bal")), P("level", None, None)),
        check_vma=False,
    )
```

time: 54.7 us -> 48.8 us (0.89)
  starting transfers between devices: 28.7 us -> 24.7 us
  waiting for transfers between devices: 16.1 us -> 14.3 us
  other arithmetic: 0.69 us -> 0.08 us
    ppermute x12 -> x9, starting transfers between devices: 20.5 us -> 15.2 us  [from_partner(): lax.ppermute(array, axis, [(i, i ^ mask) for i in range(lax.axis_size(axi...]
    ppermute x12 -> x9, waiting for transfers between devices: 12.9 us -> 7.74 us  [from_partner(): lax.ppermute(array, axis, [(i, i ^ mask) for i in range(lax.axis_size(axi...]
    all_to_all x1, waiting for transfers between devices: 3.2 us -> 6.56 us  [per_device(): lax.all_to_all(partial.reshape(levels, FINE // 4, 4, LANES), 'level', 0,...]
    all_to_all x1, starting transfers between devices: 8.24 us -> 9.51 us  [per_device(): lax.all_to_all(partial.reshape(levels, FINE // 4, 4, LANES), 'level', 0,...]
    add x1 -> x0, other arithmetic: 0.65 us -> none  [per_device(): partial = partial + from_partner(pieces[mask], 'level', mask)]
  transfers between devices with their start and end apart: 13 -> 10, of which waited for: 8 -> 5; matrix products, arithmetic and copies ran while one was open for 1% -> 0% of each run, Pallas kernels for 2% -> 10%
where the time goes in v3:
time: 48.8 us; the launch traced here: 48.5 us
  starting transfers between devices  24.7 us (51%)
  waiting for transfers between devices  14.3 us (29%)
  Pallas kernels  8.08 us (17%)
  between operations  1.36 us (3%)
    ppermute x9, starting transfers between devices, from_partner(): lax.ppermute(array, axis, [(i, i ^ mask) for i in range(lax.axis_size(axi...  15.2 us
    all_to_all x1, starting transfers between devices, per_device(): lax.all_to_all(partial.reshape(levels, FINE // 4, 4, LANES), 'level', 0,...  9.51 us
    pallas_call x6, Pallas kernels, call(): return kernel(*args)  8.08 us
    ppermute x9, waiting for transfers between devices, from_partner(): lax.ppermute(array, axis, [(i, i ^ mask) for i in range(lax.axis_size(axi...  7.74 us
    all_to_all x1, waiting for transfers between devices, per_device(): lax.all_to_all(partial.reshape(levels, FINE // 4, 4, LANES), 'level', 0,...  6.56 us
  transfers between devices with their start and end apart: 10, of which 5 were waited for; matrix products, arithmetic and copies ran while one was open for 0% of the time, Pallas kernels for 10%

profile of v3, /device:TPU:1, one launch (start us, length us, event | category | flops | bytes accessed | tf_op | source)
XLA Modules:
  0.0 48.5 jit_solution(4651531171041953009)
XLA Ops:
  1.3 2.0 %shard_map.76 = (f32[2560,128]{1,0:T(8,128)S(1)}, f32[648,128]{1,0:T(8,128)S(1)}, s32[8,128]{1,0:T(8,128)S(1)}, f32[640,128]{1,0:T(8,128)S(1)}, f32[640,128]{1,0:T(8,128)S(1)}) custom-call(s32[1]{0:T(128)S(6)} %copy.11.live, s32[3]{0:T(128)} %bitcast.26, s32[24]{0:T(128)} %ids.1, s32[6144]{0:T(1024)} %parent_of.1, f32[5,3,256,128]{3,2,1,0:T(8,128)} %bitcast.21), custom_call_target="tpu_custom_call" | custom-call | tf_op jit(solution)/shard_map/pallas_call | solution.py:274
  3.3 3.3 %collective-permute-start.4 = (f32[640,128]{1,0:T(8,128)S(1)}, f32[640,128]{1,0:T(8,128)S(1)}, u32[]{:S(2)}, u32[]{:S(2)}) collective-permute-start(f32[640,128]{1,0:T(8,128)S(1)} %get-tuple-element.20), channel_id=1, source_target_pairs={{0,1},{1,0},{2,3},{3,2},{4,5},{5,4},{6,7},{7,6},{8,9},{9,8},{10,11... | collective-permute-start | bytes 983048 | tf_op jit(solution)/shard_map/ppermute | solution.py:34
  6.6 1.3 %collective-permute-done.4.other = f32[640,128]{1,0:T(8,128)S(1)} collective-permute-done((f32[640,128]{1,0:T(8,128)S(1)}, f32[640,128]{1,0:T(8,128)S(1)}, u32[]{:S(2)}, u32[]{:S(2)}) %collective-permute-start.4) | collective-permute-done | bytes 327712 | tf_op jit(solution)/shard_map/ppermute | solution.py:34
  7.9 0.8 %shard_map.80 = f32[640,128]{1,0:T(8,128)} custom-call(f32[640,128]{1,0:T(8,128)S(1)} %get-tuple-element.19.mine, f32[640,128]{1,0:T(8,128)S(1)} %collective-permute-done.4.other), custom_call_target="tpu_custom_call" | custom-call | tf_op jit(solution)/shard_map/pallas_call | solution.py:274
  8.6 9.5 %all-to-all-start = ((f32[32,5,4,128]{3,2,1,0:T(4,128)}), f32[32,5,4,128]{3,2,1,0:T(4,128)S(1)}, u32[]{:S(2)}, u32[]{:S(2)}) async-start(f32[32,5,4,128]{3,2,1,0:T(4,128)} %bitcast.13), calls=%async_computation | async-start | bytes 655360 | tf_op jit(solution)/shard_map/all_to_all | solution.py:308
  18.1 0.7 %collective-permute-start = (f32[648,128]{1,0:T(8,128)S(1)}, f32[648,128]{1,0:T(8,128)S(1)}, u32[]{:S(2)}, u32[]{:S(2)}) collective-permute-start(f32[648,128]{1,0:T(8,128)S(1)} %get-tuple-element.13), channel_id=1, source_target_pairs={{0,1},{1,0},{2,3},{3,2},{4,5},{5,4},{6,7},{7,6},{8,9},{9,8},{10,11... | collective-permute-start | bytes 995336 | tf_op jit(solution)/shard_map/ppermute | solution.py:34
  18.9 1.3 %collective-permute-done.came = f32[648,128]{1,0:T(8,128)S(1)} collective-permute-done((f32[648,128]{1,0:T(8,128)S(1)}, f32[648,128]{1,0:T(8,128)S(1)}, u32[]{:S(2)}, u32[]{:S(2)}) %collective-permute-start) | collective-permute-done | bytes 331808 | tf_op jit(solution)/shard_map/ppermute | solution.py:34
  20.1 0.5 %shard_map.77 = (f32[648,128]{1,0:T(8,128)S(1)}, f32[648,128]{1,0:T(8,128)S(1)}) custom-call(s32[8,128]{1,0:T(8,128)S(1)} %get-tuple-element.12.info, f32[2560,128]{1,0:T(8,128)S(1)} %get-tuple-element.14.held, f32[648,128]{1,0:T(8,128)S(1)} %collective-permute-done.came), custom_call_target="tpu_custom_call" | custom-call | tf_op jit(solution)/shard_map/pallas_call | solution.py:274
  20.7 2.7 %collective-permute-start.2 = (f32[648,128]{1,0:T(8,128)S(1)}, f32[648,128]{1,0:T(8,128)S(1)}, u32[]{:S(2)}, u32[]{:S(2)}) collective-permute-start(f32[648,128]{1,0:T(8,128)S(1)} %get-tuple-element.16), channel_id=1, source_target_pairs={{0,4},{1,5},{2,6},{3,7},{4,0},{5,1},{6,2},{7,3},{8,12},{9,13},{10,... | collective-permute-start | bytes 995336 | tf_op jit(solution)/shard_map/ppermute | solution.py:34
  23.4 0.9 %collective-permute-start.3 = (f32[648,128]{1,0:T(8,128)S(1)}, f32[648,128]{1,0:T(8,128)S(1)}, u32[]{:S(2)}, u32[]{:S(2)}) collective-permute-start(f32[648,128]{1,0:T(8,128)S(1)} %get-tuple-element.15), channel_id=1, source_target_pairs={{0,6},{1,7},{2,4},{3,5},{4,2},{5,3},{6,0},{7,1},{8,14},{9,15},{10,... | collective-permute-start | bytes 995336 | tf_op jit(solution)/shard_map/ppermute | solution.py:34
  24.3 0.0 collective-permute-start.1
  24.3 6.6 %all-to-all-done = f32[32,5,4,128]{3,2,1,0:T(4,128)S(1)} async-done(((f32[32,5,4,128]{3,2,1,0:T(4,128)}), f32[32,5,4,128]{3,2,1,0:T(4,128)S(1)}, u32[]{:S(2)}, u32[]{:S(2)}) %all-to-all-start) | async-done | bytes 327712 | tf_op jit(solution)/shard_map/all_to_all | solution.py:308
  30.9 0.1 reduce_sum.9
  31.0 2.8 %collective-permute-start.7 = (f32[5,4,128]{2,1,0:T(4,128)S(1)}, f32[5,4,128]{2,1,0:T(4,128)S(1)}, u32[]{:S(2)}, u32[]{:S(2)}) collective-permute-start(f32[5,4,128]{2,1,0:T(4,128)S(1)} %reduce_sum.9), channel_id=1, source_target_pairs={{0,4},{1,5},{2,6},{3,7},{4,0},{5,1},{6,2},{7,3},{8,12},{9,13},{10,... | collective-permute-start | bytes 30728 | tf_op jit(solution)/shard_map/ppermute | solution.py:34
  33.8 0.9 %collective-permute-start.6 = (f32[5,4,128]{2,1,0:T(4,128)S(1)}, f32[5,4,128]{2,1,0:T(4,128)S(1)}, u32[]{:S(2)}, u32[]{:S(2)}) collective-permute-start(f32[5,4,128]{2,1,0:T(4,128)S(1)} %reduce_sum.9), channel_id=1, source_target_pairs={{0,6},{1,7},{2,4},{3,5},{4,2},{5,3},{6,0},{7,1},{8,14},{9,15},{10,... | collective-permute-start | bytes 30728 | tf_op jit(solution)/shard_map/ppermute | solution.py:34
  34.6 3.8 %collective-permute-done.7 = f32[5,4,128]{2,1,0:T(4,128)S(1)} collective-permute-done((f32[5,4,128]{2,1,0:T(4,128)S(1)}, f32[5,4,128]{2,1,0:T(4,128)S(1)}, u32[]{:S(2)}, u32[]{:S(2)}) %collective-permute-start.7) | collective-permute-done | bytes 10272 | tf_op jit(solution)/shard_map/ppermute | solution.py:34
  38.4 1.1 %collective-permute-start.5 = (f32[5,4,128]{2,1,0:T(4,128)S(1)}, f32[5,4,128]{2,1,0:T(4,128)S(1)}, u32[]{:S(2)}, u32[]{:S(2)}) collective-permute-start(f32[5,4,128]{2,1,0:T(4,128)S(1)} %reduce_sum.9), channel_id=1, source_target_pairs={{0,2},{1,3},{2,0},{3,1},{4,6},{5,7},{6,4},{7,5},{8,10},{9,11},{10,... | collective-permute-start | bytes 30728 | tf_op jit(solution)/shard_map/ppermute | solution.py:34
  39.5 0.0 collective-permute-done.6
  39.5 1.4 %collective-permute-done.5 = f32[5,4,128]{2,1,0:T(4,128)S(1)} collective-permute-done((f32[5,4,128]{2,1,0:T(4,128)S(1)}, f32[5,4,128]{2,1,0:T(4,128)S(1)}, u32[]{:S(2)}, u32[]{:S(2)}) %collective-permute-start.5) | collective-permute-done | bytes 10272 | tf_op jit(solution)/shard_map/ppermute | solution.py:34
  41.0 2.7 %collective-permute-start.8 = (f32[20,128]{1,0:T(8,128)S(1)}, f32[20,128]{1,0:T(8,128)S(1)}, u32[]{:S(2)}, u32[]{:S(2)}) collective-permute-start(f32[20,128]{1,0:T(8,128)S(1)} %reshape.43.mine), channel_id=1, source_target_pairs={{0,1},{1,0},{2,3},{3,2},{4,5},{5,4},{6,7},{7,6},{8,9},{9,8},{10,11... | collective-permute-start | bytes 30728 | tf_op jit(solution)/shard_map/ppermute | solution.py:34
  43.7 2.5 %shard_map.78 = f32[5,3,256,128]{3,2,1,0:T(8,128)} custom-call(s32[8,128]{1,0:T(8,128)S(1)} %get-tuple-element.12.info, f32[5,3,256,128]{3,2,1,0:T(8,128)} %bitcast.22), custom_call_target="tpu_custom_call" | custom-call | tf_op jit(solution)/shard_map/pallas_call | solution.py:274
  46.2 0.0 collective-permute-done.2.far
  46.2 0.0 collective-permute-done.3.cross
  46.2 0.0 collective-permute-done.1.near
  46.2 1.7 %shard_map.79 = (f32[5,3,32,8,128]{4,3,2,1,0:T(8,128)}, s32[1,24]{1,0:T(1,128)}) custom-call(s32[8,128]{1,0:T(8,128)S(1)} %get-tuple-element.12.info, f32[648,128]{1,0:T(8,128)S(1)} %collective-permute-done.came, f32[648,128]{1,0:T(8,128)S(1)} %collective-permute-done.1.near, ...), custom_call_target="tpu_custom_call", output_to_operand_aliasing={{0}: (5, {})} | custom-call | tf_op jit(solution)/shard_map/pallas_call | solution.py:274
  47.9 0.0 collective-permute-done.8.other
  47.9 0.6 %shard_map.81 = f32[40,128]{1,0:T(8,128)} custom-call(f32[20,128]{1,0:T(8,128)S(1)} %reshape.43.mine, f32[20,128]{1,0:T(8,128)S(1)} %collective-permute-done.8.other), custom_call_target="tpu_custom_call" | custom-call | tf_op jit(solution)/shard_map/pallas_call | solution.py:274
  (2 shorter events, 0.0 us)
Async XLA Ops:
  3.3 4.6 %collective-permute-start.4 = (f32[640,128]{1,0:T(8,128)S(1)}, f32[640,128]{1,0:T(8,128)S(1)}, u32[]{:S(2)}, u32[]{:S(2)}) collective-permute-start(f32[640,128]{1,0:T(8,128)S(1)} %get-tuple-element.20), channel_id=1, source_target_pairs={{0,1},{1,0},{2,3},{3,2},{4,5},{5,4},{6,7},{7,6},{8,9},{9,8},{10,11... | collective-permute-start | bytes 983048 | tf_op jit(solution)/shard_map/ppermute | solution.py:34
  8.6 22.3 %all-to-all-start = ((f32[32,5,4,128]{3,2,1,0:T(4,128)}), f32[32,5,4,128]{3,2,1,0:T(4,128)S(1)}, u32[]{:S(2)}, u32[]{:S(2)}) async-start(f32[32,5,4,128]{3,2,1,0:T(4,128)} %bitcast.13), calls=%async_computation | async-start | bytes 655360 | tf_op jit(solution)/shard_map/all_to_all | solution.py:308
  18.1 2.0 %collective-permute-start = (f32[648,128]{1,0:T(8,128)S(1)}, f32[648,128]{1,0:T(8,128)S(1)}, u32[]{:S(2)}, u32[]{:S(2)}) collective-permute-start(f32[648,128]{1,0:T(8,128)S(1)} %get-tuple-element.13), channel_id=1, source_target_pairs={{0,1},{1,0},{2,3},{3,2},{4,5},{5,4},{6,7},{7,6},{8,9},{9,8},{10,11... | collective-permute-start | bytes 995336 | tf_op jit(solution)/shard_map/ppermute | solution.py:34
  20.7 25.5 %collective-permute-start.2 = (f32[648,128]{1,0:T(8,128)S(1)}, f32[648,128]{1,0:T(8,128)S(1)}, u32[]{:S(2)}, u32[]{:S(2)}) collective-permute-start(f32[648,128]{1,0:T(8,128)S(1)} %get-tuple-element.16), channel_id=1, source_target_pairs={{0,4},{1,5},{2,6},{3,7},{4,0},{5,1},{6,2},{7,3},{8,12},{9,13},{10,... | collective-permute-start | bytes 995336 | tf_op jit(solution)/shard_map/ppermute | solution.py:34
  23.4 22.8 %collective-permute-start.3 = (f32[648,128]{1,0:T(8,128)S(1)}, f32[648,128]{1,0:T(8,128)S(1)}, u32[]{:S(2)}, u32[]{:S(2)}) collective-permute-start(f32[648,128]{1,0:T(8,128)S(1)} %get-tuple-element.15), channel_id=1, source_target_pairs={{0,6},{1,7},{2,4},{3,5},{4,2},{5,3},{6,0},{7,1},{8,14},{9,15},{10,... | collective-permute-start | bytes 995336 | tf_op jit(solution)/shard_map/ppermute | solution.py:34
  24.3 21.9 %collective-permute-start.1 = (f32[648,128]{1,0:T(8,128)S(1)}, f32[648,128]{1,0:T(8,128)S(1)}, u32[]{:S(2)}, u32[]{:S(2)}) collective-permute-start(f32[648,128]{1,0:T(8,128)S(1)} %get-tuple-element.15), channel_id=1, source_target_pairs={{0,2},{1,3},{2,0},{3,1},{4,6},{5,7},{6,4},{7,5},{8,10},{9,11},{10,... | collective-permute-start | bytes 995336 | tf_op jit(solution)/shard_map/ppermute | solution.py:34
  31.0 7.4 %collective-permute-start.7 = (f32[5,4,128]{2,1,0:T(4,128)S(1)}, f32[5,4,128]{2,1,0:T(4,128)S(1)}, u32[]{:S(2)}, u32[]{:S(2)}) collective-permute-start(f32[5,4,128]{2,1,0:T(4,128)S(1)} %reduce_sum.9), channel_id=1, source_target_pairs={{0,4},{1,5},{2,6},{3,7},{4,0},{5,1},{6,2},{7,3},{8,12},{9,13},{10,... | collective-permute-start | bytes 30728 | tf_op jit(solution)/shard_map/ppermute | solution.py:34
  33.8 5.7 %collective-permute-start.6 = (f32[5,4,128]{2,1,0:T(4,128)S(1)}, f32[5,4,128]{2,1,0:T(4,128)S(1)}, u32[]{:S(2)}, u32[]{:S(2)}) collective-permute-start(f32[5,4,128]{2,1,0:T(4,128)S(1)} %reduce_sum.9), channel_id=1, source_target_pairs={{0,6},{1,7},{2,4},{3,5},{4,2},{5,3},{6,0},{7,1},{8,14},{9,15},{10,... | collective-permute-start | bytes 30728 | tf_op jit(solution)/shard_map/ppermute | solution.py:34
  38.4 2.5 %collective-permute-start.5 = (f32[5,4,128]{2,1,0:T(4,128)S(1)}, f32[5,4,128]{2,1,0:T(4,128)S(1)}, u32[]{:S(2)}, u32[]{:S(2)}) collective-permute-start(f32[5,4,128]{2,1,0:T(4,128)S(1)} %reduce_sum.9), channel_id=1, source_target_pairs={{0,2},{1,3},{2,0},{3,1},{4,6},{5,7},{6,4},{7,5},{8,10},{9,11},{10,... | collective-permute-start | bytes 30728 | tf_op jit(solution)/shard_map/ppermute | solution.py:34
  41.0 7.0 %collective-permute-start.8 = (f32[20,128]{1,0:T(8,128)S(1)}, f32[20,128]{1,0:T(8,128)S(1)}, u32[]{:S(2)}, u32[]{:S(2)}) collective-permute-start(f32[20,128]{1,0:T(8,128)S(1)} %reshape.43.mine), channel_id=1, source_target_pairs={{0,1},{1,0},{2,3},{3,2},{4,5},{5,4},{6,7},{7,6},{8,9},{9,8},{10,11... | collective-permute-start | bytes 30728 | tf_op jit(solution)/shard_map/ppermute | solution.py:34

commit v4 on v3

--- a/solution.py
+++ b/solution.py
@@ -20,6 +20,7 @@
 MSG = HEAD + 8
 FINE = 20
 PAR_DEV = 2
+NEAR_LEVELS = 4
 F32 = jnp.float32
 I32 = jnp.int32
 LIVE_AT = 16
@@ -32,6 +33,10 @@
 
 def from_partner(array, axis, mask):
     return lax.ppermute(array, axis, [(i, i ^ mask) for i in range(lax.axis_size(axis))])
+
+
+def place_of(level, levels):
+    return (levels // NEAR_LEVELS - 1 - level // NEAR_LEVELS) * NEAR_LEVELS + level % NEAR_LEVELS
 
 
 def lanes():
@@ -73,8 +78,8 @@
 
 
 def load_kernel(
-    live, counts, ids, parent_of, x, held, msg, info, mine, other,
-    counts_s, ids_s, parents, weight, fine, both, sems, small_sems,
+    live, counts, ids, parent_of, x, held, info, mine, other,
+    counts_s, ids_s, parents, weight, high, low, fine, both, sems, small_sems,
 ):
     small = [
         pltpu.make_async_copy(src, dst, small_sems.at[i])
@@ -82,23 +87,15 @@
     ]
     for copy in small:
         copy.start()
-    copies = []
-    for var in range(VARS):
-        copies += block_copies(x, held, sems, range(LIVE_TILES), var, True)
-    for copy in copies:
-        copy.start()
+    copies = [block_copies(x, held, sems, range(LIVE_TILES), var, True) for var in range(VARS)]
+    for pair in copies:
+        for copy in pair:
+            copy.start()
     fill_weight(weight)
     both[...] = jnp.zeros_like(both)
     for copy in small:
         copy.wait()
-    sent = counts_s[0]
-    first = live[0] - sent
     lane = lanes()
-    head = jnp.where(lane == SEND, sent.astype(F32), 0.0)
-    for lane_id in range(SEND):
-        slot = jnp.minimum(first + lane_id, LIVE - 1)
-        head = jnp.where(lane == lane_id, ids_s[slot].astype(F32), head)
-    msg[pl.ds(HEAD, 8), :] = head
     numbers = jnp.where(lane == LIVE_AT, live[0], 0)
     for turn in range(3):
         numbers = jnp.where(lane == COUNTS_AT + turn, counts_s[turn], numbers)
@@ -109,29 +106,39 @@
         mark = ids_s[slot]
         numbers = jnp.where(lane == slot, mark, numbers)
         parent = parents[mark]
-        base = (parent // PAR_DEV) * FINE + jnp.bitwise_xor(parent % PAR_DEV, core) * half
+        base = place_of(parent // PAR_DEV, half // FINE) * FINE + jnp.bitwise_xor(parent % PAR_DEV, core) * half
         bases.append(jnp.where(slot < live[0], base, PAR_DEV * half))
     info[...] = numbers
-    for copy in copies:
-        copy.wait()
-
-    groups = LIVE_TILES * VARS * SPAN // 8
-    rows = held[...].reshape(groups, 8, TILE, LANES)
-    pieces = []
-    for side in range(4):
-        at = side // 2 * 4 + side % 2
-        pieces.append((rows[:, at] + rows[:, at + 2]).reshape(groups * TILE, LANES))
-    pairs = jnp.concatenate(pieces, axis=1)
-    high = pairs.astype(jnp.bfloat16)
-    low = (pairs - high.astype(F32)).astype(jnp.bfloat16)
+
     w = weight[...]
-    fine[...] = jnp.dot(high, w, preferred_element_type=F32) + jnp.dot(low, w, preferred_element_type=F32)
+    part = FINE // VARS * TILE
+    for var in range(VARS):
+        for copy in copies[var]:
+            copy.wait()
+        for tile in range(LIVE_TILES):
+            rows = held[pl.ds((tile * VARS + var) * SPAN * TILE, SPAN * TILE), :].reshape(-1, 8, TILE, LANES)
+            to = pl.ds((tile * VARS + var) * part, part)
+            for side in range(4):
+                at = side // 2 * 4 + side % 2
+                pairs = (rows[:, at] + rows[:, at + 2]).reshape(part, LANES)
+                near = pairs.astype(jnp.bfloat16)
+                high[to, pl.ds(side * LANES, LANES)] = near
+                low[to, pl.ds(side * LANES, LANES)] = (pairs - near.astype(F32)).astype(jnp.bfloat16)
+    fine[...] = jnp.dot(high[...], w, preferred_element_type=F32) + jnp.dot(low[...], w, preferred_element_type=F32)
     for slot, base in enumerate(bases):
         src = (slot // TILE) * (FINE * TILE) + slot % TILE
         for start, size in ((0, 8), (8, 8), (16, 4)):
             both[pl.ds(base + start, size), :] += fine[pl.ds(src + start * TILE, size, stride=TILE), :]
     mine[...] = both[pl.ds(0, half), :]
     other[...] = both[pl.ds(half, half), :]
+
+
+def message_kernel(info, held, msg):
+    lane = lanes()
+    sent = info[0, COUNTS_AT]
+    first = info[0, LIVE_AT] - sent
+    head = pltpu.roll(info[...].astype(F32), lax.rem(LANES - first, LANES), 1)
+    msg[pl.ds(HEAD, 8), :] = jnp.where(lane == SEND, sent.astype(F32), head)
     for piece in range(SEND):
 
         @pl.when(piece < sent)
@@ -283,21 +290,24 @@
     dma = pltpu.SemaphoreType.DMA
     levels = lax.axis_size("level")
     half = pltpu.VMEM((levels * FINE, LANES), F32)
-    held, first, info, mine, other = call(
+    held, info, mine, other = call(
         load_kernel,
-        (pltpu.VMEM((LIVE_TILES * TILE_ROWS, LANES), F32), message, pltpu.VMEM((8, LANES), I32), half, half),
+        (pltpu.VMEM((LIVE_TILES * TILE_ROWS, LANES), F32), pltpu.VMEM((8, LANES), I32), half, half),
         [SMEM] + [HBM] * 4,
         (live, counts, patch_ids, parent_of, x),
-        (VMEM,) * 5,
+        (VMEM,) * 4,
         [pltpu.SMEM(a.shape, I32) for a in (counts, patch_ids, parent_of)]
         + [
             pltpu.VMEM((4 * LANES, LANES), jnp.bfloat16),
+            pltpu.VMEM((LIVE_TILES * TILE * FINE, 4 * LANES), jnp.bfloat16),
+            pltpu.VMEM((LIVE_TILES * TILE * FINE, 4 * LANES), jnp.bfloat16),
             pltpu.VMEM((LIVE_TILES * TILE * FINE, LANES), F32),
             pltpu.VMEM((PAR_DEV * levels * FINE + 24, LANES), F32),
             dma((LIVE_TILES * VARS,)),
             dma((3,)),
         ],
     )
+    first = call(message_kernel, message, [VMEM, VMEM], (info, held), VMEM)
     came = from_partner(first, "bal", 1)
     last, below = call(pick_kernel, (message, message), [VMEM] * 3, (info, held, came), (VMEM, VMEM))
     partial = call(add_kernel, half, [VMEM, VMEM], (mine, from_partner(other, "bal", 1)), VMEM)
@@ -305,7 +315,10 @@
     near = from_partner(last, "bal", 2)
     cross = from_partner(last, "bal", 6)
 
-    tiles = lax.all_to_all(partial.reshape(levels, FINE // 4, 4, LANES), "level", 0, 0, tiled=True)
+    order = [place_of(level, levels) for level in range(levels)]
+    tiles = lax.all_to_all(
+        partial.reshape(levels, FINE // 4, 4, LANES), "level", 0, 0, axis_index_groups=[order], tiled=True
+    )
     sums = jnp.sum(tiles, axis=0)
     sums = sums + from_partner(sums, "bal", 2) + from_partner(sums, "bal", 6) + from_partner(sums, "bal", 4)
     sums = sums.reshape(FINE, LANES)

time: 48.8 us -> 49.5 us (1.014)
  starting transfers between devices: 24.7 us -> 25.3 us
    all_to_all x1, waiting for transfers between devices: 6.56 us -> 3.07 us  [per_device(): lax.all_to_all(partial.reshape(levels, FINE // 4, 4, LANES), 'level', 0,...]
    ppermute x9, waiting for transfers between devices: 7.74 us -> 11.1 us  [from_partner(): lax.ppermute(array, axis, [(i, i ^ mask) for i in range(lax.axis_size(axi...]
    pallas_call x6 -> x7, Pallas kernels: 8.08 us -> 8.38 us  [call(): return kernel(*args)]
where the time goes in v4:
time: 49.5 us; the launch traced here: 49.3 us
  starting transfers between devices  25.3 us (51%)
  waiting for transfers between devices  14.2 us (29%)
  Pallas kernels  8.38 us (17%)
  between operations  1.37 us (3%)
    ppermute x9, starting transfers between devices, from_partner(): lax.ppermute(array, axis, [(i, i ^ mask) for i in range(lax.axis_size(axi...  15.7 us
    ppermute x9, waiting for transfers between devices, from_partner(): lax.ppermute(array, axis, [(i, i ^ mask) for i in range(lax.axis_size(axi...  11.1 us
    all_to_all x1, starting transfers between devices, per_device(): lax.all_to_all(partial.reshape(levels, FINE // 4, 4, LANES), 'level', 0,...  9.6 us
    pallas_call x7, Pallas kernels, call(): return kernel(*args)  8.38 us
    all_to_all x1, waiting for transfers between devices, per_device(): lax.all_to_all(partial.reshape(levels, FINE // 4, 4, LANES), 'level', 0,...  3.07 us
  transfers between devices with their start and end apart: 10, of which 5 were waited for; matrix products, arithmetic and copies ran while one was open for 0% of the time, Pallas kernels for 10%

profile of v4, /device:TPU:1, one launch (start us, length us, event | category | flops | bytes accessed | tf_op | source)
XLA Modules:
  0.0 49.3 jit_solution(228257894385519131)
XLA Ops:
  1.3 2.0 %shard_map.76 = (f32[2560,128]{1,0:T(8,128)S(1)}, s32[8,128]{1,0:T(8,128)S(1)}, f32[640,128]{1,0:T(8,128)S(1)}, f32[640,128]{1,0:T(8,128)S(1)}) custom-call(s32[1]{0:T(128)S(6)} %copy.11.live, s32[3]{0:T(128)} %bitcast.26, s32[24]{0:T(128)} %ids.1, s32[6144]{0:T(1024)} %parent_of.1, f32[5,3,256,128]{3,2,1,0:T(8,128)} %bitcast.21), custom_call_target="tpu_custom_call" | custom-call | tf_op jit(solution)/shard_map/pallas_call | solution.py:281
  3.3 3.3 %collective-permute-start.4 = (f32[640,128]{1,0:T(8,128)S(1)}, f32[640,128]{1,0:T(8,128)S(1)}, u32[]{:S(2)}, u32[]{:S(2)}) collective-permute-start(f32[640,128]{1,0:T(8,128)S(1)} %get-tuple-element.18), channel_id=1, source_target_pairs={{0,1},{1,0},{2,3},{3,2},{4,5},{5,4},{6,7},{7,6},{8,9},{9,8},{10,11... | collective-permute-start | bytes 983048 | tf_op jit(solution)/shard_map/ppermute | solution.py:35
  6.6 1.3 %collective-permute-done.4.other = f32[640,128]{1,0:T(8,128)S(1)} collective-permute-done((f32[640,128]{1,0:T(8,128)S(1)}, f32[640,128]{1,0:T(8,128)S(1)}, u32[]{:S(2)}, u32[]{:S(2)}) %collective-permute-start.4) | collective-permute-done | bytes 327712 | tf_op jit(solution)/shard_map/ppermute | solution.py:35
  7.9 0.8 %shard_map.81 = f32[640,128]{1,0:T(8,128)} custom-call(f32[640,128]{1,0:T(8,128)S(1)} %get-tuple-element.17.mine, f32[640,128]{1,0:T(8,128)S(1)} %collective-permute-done.4.other), custom_call_target="tpu_custom_call" | custom-call | tf_op jit(solution)/shard_map/pallas_call | solution.py:281
  8.6 9.6 %all-to-all-start = ((f32[32,5,4,128]{3,2,1,0:T(4,128)}), f32[32,5,4,128]{3,2,1,0:T(4,128)S(1)}, u32[]{:S(2)}, u32[]{:S(2)}) async-start(f32[32,5,4,128]{3,2,1,0:T(4,128)} %bitcast.13), calls=%async_computation | async-start | bytes 655360 | tf_op jit(solution)/shard_map/all_to_all | solution.py:319
  18.2 0.3 shard_map.77
  18.5 1.0 %collective-permute-start = (f32[648,128]{1,0:T(8,128)S(1)}, f32[648,128]{1,0:T(8,128)S(1)}, u32[]{:S(2)}, u32[]{:S(2)}) collective-permute-start(f32[648,128]{1,0:T(8,128)S(1)} %shard_map.77), channel_id=1, source_target_pairs={{0,1},{1,0},{2,3},{3,2},{4,5},{5,4},{6,7},{7,6},{8,9},{9,8},{10,11... | collective-permute-start | bytes 995336 | tf_op jit(solution)/shard_map/ppermute | solution.py:35
  19.5 1.3 %collective-permute-done.came = f32[648,128]{1,0:T(8,128)S(1)} collective-permute-done((f32[648,128]{1,0:T(8,128)S(1)}, f32[648,128]{1,0:T(8,128)S(1)}, u32[]{:S(2)}, u32[]{:S(2)}) %collective-permute-start) | collective-permute-done | bytes 331808 | tf_op jit(solution)/shard_map/ppermute | solution.py:35
  20.8 0.5 %shard_map.78 = (f32[648,128]{1,0:T(8,128)S(1)}, f32[648,128]{1,0:T(8,128)S(1)}) custom-call(s32[8,128]{1,0:T(8,128)S(1)} %get-tuple-element.11.info, f32[2560,128]{1,0:T(8,128)S(1)} %get-tuple-element.12.held, f32[648,128]{1,0:T(8,128)S(1)} %collective-permute-done.came), custom_call_target="tpu_custom_call" | custom-call | tf_op jit(solution)/shard_map/pallas_call | solution.py:281
  21.3 2.7 %collective-permute-start.2 = (f32[648,128]{1,0:T(8,128)S(1)}, f32[648,128]{1,0:T(8,128)S(1)}, u32[]{:S(2)}, u32[]{:S(2)}) collective-permute-start(f32[648,128]{1,0:T(8,128)S(1)} %get-tuple-element.14), channel_id=1, source_target_pairs={{0,4},{1,5},{2,6},{3,7},{4,0},{5,1},{6,2},{7,3},{8,12},{9,13},{10,... | collective-permute-start | bytes 995336 | tf_op jit(solution)/shard_map/ppermute | solution.py:35
  24.1 1.0 %collective-permute-start.3 = (f32[648,128]{1,0:T(8,128)S(1)}, f32[648,128]{1,0:T(8,128)S(1)}, u32[]{:S(2)}, u32[]{:S(2)}) collective-permute-start(f32[648,128]{1,0:T(8,128)S(1)} %get-tuple-element.13), channel_id=1, source_target_pairs={{0,6},{1,7},{2,4},{3,5},{4,2},{5,3},{6,0},{7,1},{8,14},{9,15},{10,... | collective-permute-start | bytes 995336 | tf_op jit(solution)/shard_map/ppermute | solution.py:35
  25.1 0.0 collective-permute-start.1
  25.1 3.1 %all-to-all-done = f32[32,5,4,128]{3,2,1,0:T(4,128)S(1)} async-done(((f32[32,5,4,128]{3,2,1,0:T(4,128)}), f32[32,5,4,128]{3,2,1,0:T(4,128)S(1)}, u32[]{:S(2)}, u32[]{:S(2)}) %all-to-all-start) | async-done | bytes 327712 | tf_op jit(solution)/shard_map/all_to_all | solution.py:319
  28.1 0.1 reduce_sum.9
  28.2 2.8 %collective-permute-start.7 = (f32[5,4,128]{2,1,0:T(4,128)S(1)}, f32[5,4,128]{2,1,0:T(4,128)S(1)}, u32[]{:S(2)}, u32[]{:S(2)}) collective-permute-start(f32[5,4,128]{2,1,0:T(4,128)S(1)} %reduce_sum.9), channel_id=1, source_target_pairs={{0,4},{1,5},{2,6},{3,7},{4,0},{5,1},{6,2},{7,3},{8,12},{9,13},{10,... | collective-permute-start | bytes 30728 | tf_op jit(solution)/shard_map/ppermute | solution.py:35
  31.0 0.9 %collective-permute-start.6 = (f32[5,4,128]{2,1,0:T(4,128)S(1)}, f32[5,4,128]{2,1,0:T(4,128)S(1)}, u32[]{:S(2)}, u32[]{:S(2)}) collective-permute-start(f32[5,4,128]{2,1,0:T(4,128)S(1)} %reduce_sum.9), channel_id=1, source_target_pairs={{0,6},{1,7},{2,4},{3,5},{4,2},{5,3},{6,0},{7,1},{8,14},{9,15},{10,... | collective-permute-start | bytes 30728 | tf_op jit(solution)/shard_map/ppermute | solution.py:35
  31.9 7.2 %collective-permute-done.7 = f32[5,4,128]{2,1,0:T(4,128)S(1)} collective-permute-done((f32[5,4,128]{2,1,0:T(4,128)S(1)}, f32[5,4,128]{2,1,0:T(4,128)S(1)}, u32[]{:S(2)}, u32[]{:S(2)}) %collective-permute-start.7) | collective-permute-done | bytes 10272 | tf_op jit(solution)/shard_map/ppermute | solution.py:35
  39.1 1.1 %collective-permute-start.5 = (f32[5,4,128]{2,1,0:T(4,128)S(1)}, f32[5,4,128]{2,1,0:T(4,128)S(1)}, u32[]{:S(2)}, u32[]{:S(2)}) collective-permute-start(f32[5,4,128]{2,1,0:T(4,128)S(1)} %reduce_sum.9), channel_id=1, source_target_pairs={{0,2},{1,3},{2,0},{3,1},{4,6},{5,7},{6,4},{7,5},{8,10},{9,11},{10,... | collective-permute-start | bytes 30728 | tf_op jit(solution)/shard_map/ppermute | solution.py:35
  40.2 0.0 collective-permute-done.6
  40.2 1.4 %collective-permute-done.5 = f32[5,4,128]{2,1,0:T(4,128)S(1)} collective-permute-done((f32[5,4,128]{2,1,0:T(4,128)S(1)}, f32[5,4,128]{2,1,0:T(4,128)S(1)}, u32[]{:S(2)}, u32[]{:S(2)}) %collective-permute-start.5) | collective-permute-done | bytes 10272 | tf_op jit(solution)/shard_map/ppermute | solution.py:35
  41.6 2.8 %collective-permute-start.8 = (f32[20,128]{1,0:T(8,128)S(1)}, f32[20,128]{1,0:T(8,128)S(1)}, u32[]{:S(2)}, u32[]{:S(2)}) collective-permute-start(f32[20,128]{1,0:T(8,128)S(1)} %reshape.43.mine), channel_id=1, source_target_pairs={{0,1},{1,0},{2,3},{3,2},{4,5},{5,4},{6,7},{7,6},{8,9},{9,8},{10,11... | collective-permute-start | bytes 30728 | tf_op jit(solution)/shard_map/ppermute | solution.py:35
  44.4 2.5 %shard_map.79 = f32[5,3,256,128]{3,2,1,0:T(8,128)} custom-call(s32[8,128]{1,0:T(8,128)S(1)} %get-tuple-element.11.info, f32[5,3,256,128]{3,2,1,0:T(8,128)} %bitcast.22), custom_call_target="tpu_custom_call" | custom-call | tf_op jit(solution)/shard_map/pallas_call | solution.py:281
  46.9 0.0 collective-permute-done.2.far
  46.9 0.0 collective-permute-done.3.cross
  46.9 0.0 collective-permute-done.1.near
  46.9 1.7 %shard_map.80 = (f32[5,3,32,8,128]{4,3,2,1,0:T(8,128)}, s32[1,24]{1,0:T(1,128)}) custom-call(s32[8,128]{1,0:T(8,128)S(1)} %get-tuple-element.11.info, f32[648,128]{1,0:T(8,128)S(1)} %collective-permute-done.came, f32[648,128]{1,0:T(8,128)S(1)} %collective-permute-done.1.near, ...), custom_call_target="tpu_custom_call", output_to_operand_aliasing={{0}: (5, {})} | custom-call | tf_op jit(solution)/shard_map/pallas_call | solution.py:281
  48.6 0.0 collective-permute-done.8.other
  48.6 0.6 %shard_map.82 = f32[40,128]{1,0:T(8,128)} custom-call(f32[20,128]{1,0:T(8,128)S(1)} %reshape.43.mine, f32[20,128]{1,0:T(8,128)S(1)} %collective-permute-done.8.other), custom_call_target="tpu_custom_call" | custom-call | tf_op jit(solution)/shard_map/pallas_call | solution.py:281
  (2 shorter events, 0.0 us)
Async XLA Ops:
  3.3 4.6 %collective-permute-start.4 = (f32[640,128]{1,0:T(8,128)S(1)}, f32[640,128]{1,0:T(8,128)S(1)}, u32[]{:S(2)}, u32[]{:S(2)}) collective-permute-start(f32[640,128]{1,0:T(8,128)S(1)} %get-tuple-element.18), channel_id=1, source_target_pairs={{0,1},{1,0},{2,3},{3,2},{4,5},{5,4},{6,7},{7,6},{8,9},{9,8},{10,11... | collective-permute-start | bytes 983048 | tf_op jit(solution)/shard_map/ppermute | solution.py:35
  8.6 19.5 %all-to-all-start = ((f32[32,5,4,128]{3,2,1,0:T(4,128)}), f32[32,5,4,128]{3,2,1,0:T(4,128)S(1)}, u32[]{:S(2)}, u32[]{:S(2)}) async-start(f32[32,5,4,128]{3,2,1,0:T(4,128)} %bitcast.13), calls=%async_computation | async-start | bytes 655360 | tf_op jit(solution)/shard_map/all_to_all | solution.py:319
  18.5 2.3 %collective-permute-start = (f32[648,128]{1,0:T(8,128)S(1)}, f32[648,128]{1,0:T(8,128)S(1)}, u32[]{:S(2)}, u32[]{:S(2)}) collective-permute-start(f32[648,128]{1,0:T(8,128)S(1)} %shard_map.77), channel_id=1, source_target_pairs={{0,1},{1,0},{2,3},{3,2},{4,5},{5,4},{6,7},{7,6},{8,9},{9,8},{10,11... | collective-permute-start | bytes 995336 | tf_op jit(solution)/shard_map/ppermute | solution.py:35
  21.3 25.5 %collective-permute-start.2 = (f32[648,128]{1,0:T(8,128)S(1)}, f32[648,128]{1,0:T(8,128)S(1)}, u32[]{:S(2)}, u32[]{:S(2)}) collective-permute-start(f32[648,128]{1,0:T(8,128)S(1)} %get-tuple-element.14), channel_id=1, source_target_pairs={{0,4},{1,5},{2,6},{3,7},{4,0},{5,1},{6,2},{7,3},{8,12},{9,13},{10,... | collective-permute-start | bytes 995336 | tf_op jit(solution)/shard_map/ppermute | solution.py:35
  24.1 22.8 %collective-permute-start.3 = (f32[648,128]{1,0:T(8,128)S(1)}, f32[648,128]{1,0:T(8,128)S(1)}, u32[]{:S(2)}, u32[]{:S(2)}) collective-permute-start(f32[648,128]{1,0:T(8,128)S(1)} %get-tuple-element.13), channel_id=1, source_target_pairs={{0,6},{1,7},{2,4},{3,5},{4,2},{5,3},{6,0},{7,1},{8,14},{9,15},{10,... | collective-permute-start | bytes 995336 | tf_op jit(solution)/shard_map/ppermute | solution.py:35
  25.1 21.8 %collective-permute-start.1 = (f32[648,128]{1,0:T(8,128)S(1)}, f32[648,128]{1,0:T(8,128)S(1)}, u32[]{:S(2)}, u32[]{:S(2)}) collective-permute-start(f32[648,128]{1,0:T(8,128)S(1)} %get-tuple-element.13), channel_id=1, source_target_pairs={{0,2},{1,3},{2,0},{3,1},{4,6},{5,7},{6,4},{7,5},{8,10},{9,11},{10,... | collective-permute-start | bytes 995336 | tf_op jit(solution)/shard_map/ppermute | solution.py:35
  28.2 10.9 %collective-permute-start.7 = (f32[5,4,128]{2,1,0:T(4,128)S(1)}, f32[5,4,128]{2,1,0:T(4,128)S(1)}, u32[]{:S(2)}, u32[]{:S(2)}) collective-permute-start(f32[5,4,128]{2,1,0:T(4,128)S(1)} %reduce_sum.9), channel_id=1, source_target_pairs={{0,4},{1,5},{2,6},{3,7},{4,0},{5,1},{6,2},{7,3},{8,12},{9,13},{10,... | collective-permute-start | bytes 30728 | tf_op jit(solution)/shard_map/ppermute | solution.py:35
  31.0 9.2 %collective-permute-start.6 = (f32[5,4,128]{2,1,0:T(4,128)S(1)}, f32[5,4,128]{2,1,0:T(4,128)S(1)}, u32[]{:S(2)}, u32[]{:S(2)}) collective-permute-start(f32[5,4,128]{2,1,0:T(4,128)S(1)} %reduce_sum.9), channel_id=1, source_target_pairs={{0,6},{1,7},{2,4},{3,5},{4,2},{5,3},{6,0},{7,1},{8,14},{9,15},{10,... | collective-permute-start | bytes 30728 | tf_op jit(solution)/shard_map/ppermute | solution.py:35
  39.1 2.5 %collective-permute-start.5 = (f32[5,4,128]{2,1,0:T(4,128)S(1)}, f32[5,4,128]{2,1,0:T(4,128)S(1)}, u32[]{:S(2)}, u32[]{:S(2)}) collective-permute-start(f32[5,4,128]{2,1,0:T(4,128)S(1)} %reduce_sum.9), channel_id=1, source_target_pairs={{0,2},{1,3},{2,0},{3,1},{4,6},{5,7},{6,4},{7,5},{8,10},{9,11},{10,... | collective-permute-start | bytes 30728 | tf_op jit(solution)/shard_map/ppermute | solution.py:35
  41.6 7.0 %collective-permute-start.8 = (f32[20,128]{1,0:T(8,128)S(1)}, f32[20,128]{1,0:T(8,128)S(1)}, u32[]{:S(2)}, u32[]{:S(2)}) collective-permute-start(f32[20,128]{1,0:T(8,128)S(1)} %reshape.43.mine), channel_id=1, source_target_pairs={{0,1},{1,0},{2,3},{3,2},{4,5},{5,4},{6,7},{7,6},{8,9},{9,8},{10,11... | collective-permute-start | bytes 30728 | tf_op jit(solution)/shard_map/ppermute | solution.py:35
